TPU v7x, 256 devices: a whole 4x4x8 slice. The times are simulated.
256 devices in a mesh: tok: 32 (over y, z_hi, core), cand: 8 (over x, z_lo).
Axes of the slice: x: 4, y: 4, z: 8 (z_hi: 4, z_lo: 2; z = z_hi * 2 + z_lo), core: 2. Of those that a mesh axis runs over, the one named last changes fastest.
Arguments:
- dec_hidden: bfloat16 [2, 64, 32, 2048], P(None, 'cand'), may hold values from -6 to 6
- enc_keys: bfloat16 [2, 4096, 2048], P(None, 'tok'), may hold values from -250 to 250
- enc_values: bfloat16 [2, 4096, 2048], P(None, 'tok'), may hold values from -72 to 72
- enc_lengths: int32 [2], replicated, may hold values from 1024 to 4096, as said below
- cand_counts: int32 [2], replicated, may hold values from 16 to 64, as said below
- gold_ids: int32 [2, 64, 32], P(None, 'cand'), may hold values from 0 to 32127
- gain_cross: float32 [2048], replicated, may hold values from 0.25 to 1.75
- w_query: bfloat16 [2048, 2048], P('cand', 'tok'), may hold values from -0.125 to 0.125
- w_out: bfloat16 [2048, 2048], P('tok', 'cand'), may hold values from -0.125 to 0.125
- gain_ffn: float32 [2048], replicated, may hold values from 0.25 to 1.75
- w_in_gate: bfloat16 [2048, 5120], P('cand', 'tok'), may hold values from -0.125 to 0.125
- w_in_up: bfloat16 [2048, 5120], P('cand', 'tok'), may hold values from -0.125 to 0.125
- w_ffn_out: bfloat16 [5120, 2048], P('tok', 'cand'), may hold values from -0.25 to 0.25
- gain_final: float32 [2048], replicated, may hold values from 0.25 to 1.75
- w_vocab: bfloat16 [2048, 32128], P('cand', 'tok'), may hold values from -20 to 20
Outputs:
- cand_scores: float32 [2, 64], P(None, 'cand')
- best_score: float32 [2], replicated
Inputs may be any that keep to these rules, and one draw needn't show every extreme that they name: `enc_lengths`: some query has all 4096 encoder tokens live. `cand_counts`: some query has all 64 candidates live.
All inputs are finite; a program needn't handle non-finite values.
Results may differ from a plain program's by a relative error of at most 0.0014.
The roundings to bfloat16 on the way count: a program that leaves them out, or rounds other values in their place, can miss the bound.
Values may be sent and summed in bfloat16 or wider, within the bound.
A program may use at most 64 MiB of HBM per device.

v0:
```python
import jax
import jax.numpy as jnp
from jax import lax
from jax.sharding import PartitionSpec as P

HEADS = 32
HEAD_DIM = 64


norm_eps = 0.25


def from_everyone(shard, axis):
    length = lax.axis_size(axis)
    return lax.all_to_all(
        jnp.broadcast_to(shard[None], (length, *shard.shape)), axis, 0, 0, tiled=True
    )


def laid_out(tiles, dim):
    tiles = jnp.moveaxis(tiles, 0, dim)
    lengths = tiles.shape
    return tiles.reshape(*lengths[:dim], lengths[dim] * lengths[dim + 1], *lengths[dim + 2 :])


def gather_directly(shard, axis, dim):
    tiles = from_everyone(shard, axis)
    return laid_out(tiles, dim)


def side_by_side(arrays, axis, split_dim, concat_dim, along):
    widths = [a.shape[along] for a in arrays]
    both = jnp.concatenate(arrays, axis=along)
    result = lax.all_to_all(both, axis, split_axis=split_dim, concat_axis=concat_dim, tiled=True)
    return tuple(jnp.split(result, [sum(widths[:k]) for k in range(1, len(widths))], axis=along))


def side_by_side_2(arrays, axis, dim, along):
    ends, at = ([], 0)
    for a in arrays[:-1]:
        at += a.shape[along]
        ends.append(at)
    both = jnp.concatenate(arrays, axis=along)
    return tuple(jnp.split(lax.all_gather(both, axis, axis=dim, tiled=True), ends, axis=along))


def all_in_one(shard, axis):
    leaves = jax.tree.leaves(shard)
    turns = sorted(range(len(leaves)), key=lambda k: -leaves[k].size)
    width = (1, *leaves[turns[0]].shape)[-1]
    lines = [
        jnp.pad(leaves[k].reshape(-1), (0, -leaves[k].size % width)).reshape(-1, width)
        for k in turns
    ]
    both, at, found = (from_everyone(jnp.concatenate(lines), axis), 0, {})
    for k, line in zip(turns, lines):
        piece = both[:, at : at + len(line)].reshape(len(both), -1)
        found[k] = piece[:, : leaves[k].size].reshape(-1, *leaves[k].shape)
        at += len(line)
    numbers = iter(range(len(leaves)))
    return jax.tree.map(lambda _: found[next(numbers)], shard)


def joined_by_halves(pieces, combine):
    while len(jax.tree.leaves(pieces)[0]) > 1:
        pieces = jax.vmap(combine)(
            *(jax.tree.map(lambda part: part[side::2], pieces) for side in (0, 1))
        )
    return jax.tree.map(lambda part: part[0], pieces)


def joined_all(shard, axis, combine):
    pieces = all_in_one(shard, axis)
    return joined_by_halves(pieces, combine)


def taken_together(shard, axis):
    everything = from_everyone(shard, axis)
    return jnp.max(everything, axis=0)


def root_norm(values, gain):
    squares = jnp.mean(values * values, axis=-1, keepdims=True)
    return values * lax.rsqrt(squares + norm_eps) * gain


def add_rows(left_side, piece):
    return jnp.dot(left_side, piece, preferred_element_type=jnp.float32)


def body(
    dec_hidden,
    enc_keys,
    enc_values,
    enc_lengths,
    cand_counts,
    gold_ids,
    gain_cross,
    w_query,
    w_out,
    gain_ffn,
    w_in_gate,
    w_in_up,
    w_ffn_out,
    gain_final,
    w_vocab,
):
    query_count, cand_dev, length_tok, model_width = dec_hidden.shape
    src_dev = enc_keys.shape[1]
    tok_count = lax.axis_size("tok")
    tok_index = lax.axis_index("tok")
    row_count = query_count * cand_dev * length_tok
    per_query = cand_dev * length_tok
    row_share = row_count // tok_count
    head_cols = w_query.shape[1]
    heads_dev = head_cols // HEAD_DIM
    inputs_flat = dec_hidden.reshape(row_count, model_width)
    normed = root_norm(inputs_flat.astype(jnp.float32), gain_cross).astype(jnp.bfloat16)
    query_local = add_rows(normed, gather_directly(w_query, "cand", 0)).astype(jnp.bfloat16)
    key_split = enc_keys.reshape(query_count, src_dev, HEADS, HEAD_DIM)
    value_split = enc_values.reshape(query_count, src_dev, HEADS, HEAD_DIM)
    keys_heads, values_heads = side_by_side((key_split, value_split), "tok", 2, 1, 0)
    total_src = src_dev * tok_count
    query_split = query_local.reshape(query_count, per_query, heads_dev, HEAD_DIM)
    live_keys = lax.iota(jnp.int32, total_src)[None, :] < enc_lengths[:, None]
    scores = jnp.einsum(
        "brhd,bshd->bhrs", query_split, keys_heads, preferred_element_type=jnp.float32
    )
    scores = jnp.where(live_keys[:, None, None, :], scores, -1e30)
    row_max = jnp.max(scores, axis=-1, keepdims=True)
    weights = jnp.where(live_keys[:, None, None, :], jnp.exp(scores - row_max), 0.0)
    denominator = jnp.sum(weights, axis=-1)
    mixed_values = jnp.einsum(
        "bhrs,bshd->brhd",
        weights.astype(jnp.bfloat16),
        values_heads,
        preferred_element_type=jnp.float32,
    )
    attended = (
        (mixed_values / denominator.transpose(0, 2, 1)[..., None])
        .reshape(row_count, head_cols)
        .astype(jnp.bfloat16)
    )
    cross_terms = jnp.dot(
        attended, gather_directly(w_out, "cand", 1), preferred_element_type=jnp.float32
    )
    cross_mine = lax.psum_scatter(cross_terms, "tok", scatter_dimension=0, tiled=True)
    inputs_mine = lax.dynamic_slice_in_dim(inputs_flat, tok_index * row_share, row_share, 0).astype(
        jnp.float32
    )
    after_cross = inputs_mine + cross_mine
    normed_ffn = root_norm(after_cross, gain_ffn).astype(jnp.bfloat16)
    ffn_every = lax.all_gather(normed_ffn, "tok", axis=0, tiled=True)
    pieces = side_by_side_2((w_in_gate, w_in_up), "cand", 0, 1)
    gate_part = add_rows(ffn_every, pieces[0])
    up_part = add_rows(ffn_every, pieces[1])
    hidden = (jax.nn.gelu(gate_part, approximate=True) * up_part).astype(jnp.bfloat16)
    ffn_terms = jnp.dot(
        hidden, gather_directly(w_ffn_out, "cand", 1), preferred_element_type=jnp.float32
    )
    after_ffn = after_cross + lax.psum_scatter(
        ffn_terms.astype(jnp.bfloat16), "tok", scatter_dimension=0, tiled=True
    ).astype(jnp.float32)
    normed_final = root_norm(after_ffn, gain_final).astype(jnp.bfloat16)
    final_every = lax.all_gather(normed_final, "tok", axis=0, tiled=True)
    vocab_cols = w_vocab.shape[1]
    logits = add_rows(final_every, lax.all_gather(w_vocab, "cand", axis=0, tiled=True))
    gold_flat = gold_ids.reshape(row_count)
    vocab_start = tok_index * vocab_cols
    matches = lax.iota(jnp.int32, vocab_cols)[None, :] == (gold_flat - vocab_start)[:, None]
    gold_local = jnp.sum(jnp.where(matches, logits, 0.0), axis=1)
    local_max = jnp.max(logits, axis=1)
    local_sum = jnp.sum(jnp.exp(logits - local_max[:, None]), axis=1)

    def combine(first, second):
        larger = jnp.maximum(first[0], second[0])
        summed = first[1] * jnp.exp(first[0] - larger) + second[1] * jnp.exp(second[0] - larger)
        return (larger, summed, first[2] + second[2])

    global_max, sum_exp, gold_logit = joined_all((local_max, local_sum, gold_local), "tok", combine)
    logprob = gold_logit - global_max - jnp.log(sum_exp)
    per_cand = jnp.mean(logprob.reshape(query_count, cand_dev, length_tok), axis=2)
    cand_index = lax.axis_index("cand") * cand_dev + lax.iota(jnp.int32, cand_dev)
    valid_cand = cand_index[None, :] < cand_counts[:, None]
    cand_scores = jnp.where(valid_cand, per_cand, 0.0)
    best_local = jnp.max(jnp.where(valid_cand, per_cand, -1e30), axis=1)
    best_score = taken_together(best_local, "cand")
    return (cand_scores, best_score)


def solution(mesh):
    in_specs = (
        P(None, "cand", None, None),
        P(None, "tok", None),
        P(None, "tok", None),
        P(),
        P(),
        P(None, "cand", None),
        P(),
        P("cand", "tok"),
        P("tok", "cand"),
        P(),
        P("cand", "tok"),
        P("cand", "tok"),
        P("tok", "cand"),
        P(),
        P("cand", "tok"),
    )
    out_specs = (P(None, "cand"), P())
    return jax.shard_map(body, mesh=mesh, in_specs=in_specs, out_specs=out_specs, check_vma=False)
```

profile of v0, /device:TPU:1, one launch (start us, length us, event | category | flops | bytes accessed | tf_op | source)
XLA Modules:
  0.0 499.6 jit_solution(5765701800943012095)
XLA Ops:
  8.0 0.9 broadcast_in_dim.39
  8.9 12.2 %all_to_all.41 = bf16[8,256,64]{1,2,0:T(8,128)(2,1)S(1)} all-to-all(bf16[8,256,64]{1,2,0:T(8,128)(2,1)S(1)} %broadcast_in_dim.39), channel_id=1, replica_groups=mesh['tok'=32,'cand'=8] {'cand'}, dimensions={0} | all-to-all | bytes 524288 | tf_op jit(solution)/shard_map/all_to_all | solution.py:15
  21.1 1.5 broadcast_in_dim.42
  22.6 4.0 all-to-all-start.2
  26.6 0.7 copy.65
  27.3 0.7 copy.66
  28.0 0.2 pad_maximum_fusion
  28.2 1.5 copy.67
  29.7 3.1 all-to-all-done.2
  32.8 13.6 %all-to-all-start = ((bf16[4,128,32,64]{1,3,0,2:T(8,128)(2,1)}), bf16[4,128,32,64]{1,3,0,2:T(8,128)(2,1)}, u32[]{:S(2)}, u32[]{:S(2)}) async-start(bf16[4,128,32,64]{1,3,0,2:T(8,128)(2,1)} %copy.67), calls=%async_computation | async-start | bytes 4194304 | tf_op jit(solution)/shard_map/all_to_all | solution.py:34
  46.4 0.0 reduce-scatter.3.cloned.1.call-start
  46.5 0.5 fusion.2
  47.0 0.1 copy-done.7
  47.1 0.5 fusion.4
  47.7 0.1 copy-done.11
  47.8 0.1 iota_compare_fusion.1
  47.9 1.0 copy.84
  48.8 0.8 convolution_convert_fusion.1
  49.6 48.7 %all-to-all-done = bf16[4,128,32,64]{1,3,0,2:T(8,128)(2,1)} async-done(((bf16[4,128,32,64]{1,3,0,2:T(8,128)(2,1)}), bf16[4,128,32,64]{1,3,0,2:T(8,128)(2,1)}, u32[]{:S(2)}, u32[]{:S(2)}) %all-to-all-start) | async-done | bytes 2097184 | tf_op jit(solution)/shard_map/all_to_all | solution.py:34
  98.3 2.8 fusion.59
  101.1 1.7 copy.70
  102.8 1.5 reshape.173
  104.3 4.5 fusion.43
  108.8 3.6 fusion.61
  112.4 1.9 copy.68
  114.3 1.3 reshape.170
  115.6 10.6 %fusion.19 = bf16[2,256,1,64]{1,3,0,2:T(8,128)(2,1)S(1)} fusion(bf16[2,4096,64]{1,2,0:T(8,128)(2,1)} %reshape.170, f32[2,256,4096]{2,1,0:T(8,128)} %fusion.43, pred[2,4096]{1,0:T(4,128)(4,1)S(1)} %iota_compare_fusion.1, f32[2,256]{1,0:T(2,128)S(1)} %fusion.61), kind=kOutput, calls=%fused_computation.24 | convolution fusion | flops 276894208 | bytes 9512960 | tf_op jit(solution)/shard_map/bhrs,bshd->brhd/dot_general | solution.py:133
  126.3 0.1 copy.72
  126.4 2.7 fusion.65
  129.0 0.0 reduce-scatter.3.cloned.1.call-update
  129.1 0.0 all-gather.7.cloned.1.call-start
  129.1 0.8 copy-done.4
  129.9 0.0 copy-done.5
  130.0 0.7 pad_maximum_fusion.1
  130.7 0.0 all-gather.5.cloned.1.call-start
  130.7 90.5 %reduce-scatter.3.cloned.1.call-done = f32[16,2048]{1,0:T(8,128)} async-done(((f32[512,2048]{1,0:T(8,128)}), f32[16,2048]{1,0:T(8,128)}) %reduce-scatter.3.cloned.1.call-update) | async-done | bytes 131088 | tf_op jit(solution)/shard_map/reduce_scatter | solution.py:147
  221.2 1.0 multiply_reduce_fusion.1
  222.3 1.6 multiply_convert_fusion.1
  223.9 0.0 reduce-scatter.5.cloned.1.call-start
  224.0 12.2 %all_to_all.42 = bf16[8,160,256]{2,1,0:T(8,128)(2,1)S(1)} all-to-all(bf16[8,160,256]{2,1,0:T(8,128)(2,1)S(1)} %broadcast_in_dim.44), channel_id=1, replica_groups=mesh['tok'=32,'cand'=8] {'cand'}, dimensions={0} | all-to-all | bytes 1310720 | tf_op jit(solution)/shard_map/all_to_all | solution.py:15
  236.2 0.1 copy.85
  236.3 0.0 all-gather.7.cloned.1.call-done
  236.3 42.3 %all-gather.5.cloned.1.call-done = bf16[512,2048]{1,0:T(8,128)(2,1)} async-done(((bf16[16,2048]{1,0:T(8,128)(2,1)}), bf16[512,2048]{1,0:T(8,128)(2,1)}) %all-gather.5.cloned.1.call-update) | async-done | bytes 2097168 | tf_op jit(solution)/shard_map/all_gather | solution.py:153
  278.6 2.6 fusion.32
  281.3 4.6 convolution_convert_fusion
  285.9 0.0 all-gather.11.cloned.1.call-start
  286.0 0.5 all-gather.11.cloned.1.call-update
  286.5 0.0 all-gather.9.cloned.1.call-start
  286.6 111.8 %reduce-scatter.5.cloned.1.call-done = bf16[16,2048]{1,0:T(8,128)(2,1)} async-done(((bf16[512,2048]{1,0:T(8,128)(2,1)}), bf16[16,2048]{1,0:T(8,128)(2,1)}) %reduce-scatter.5.cloned.1.call-update) | async-done | bytes 65552 | tf_op jit(solution)/shard_map/reduce_scatter | solution.py:161
  398.4 1.0 multiply_reduce_fusion
  399.4 1.6 multiply_convert_fusion
  401.0 0.1 sub.86
  401.1 54.7 %all-gather.9.cloned.1.call-done = bf16[512,2048]{1,0:T(8,128)(2,1)} async-done(((bf16[16,2048]{1,0:T(8,128)(2,1)}), bf16[512,2048]{1,0:T(8,128)(2,1)}) %all-gather.9.cloned.1.call-update) | async-done | bytes 2097168 | tf_op jit(solution)/shard_map/all_gather | solution.py:165
  455.8 5.1 %fusion.64 = (f32[512]{0:T(512)S(1)}, f32[512,1004]{0,1:T(8,128)S(1)}) fusion(bf16[512,2048]{1,0:T(8,128)(2,1)} %all-gather.9.cloned.1.call-done, bf16[2048,1004]{0,1:T(8,128)(2,1)} %all-gather.11.cloned.1.call-done), kind=kOutput, calls=%fused_computation.82 | convolution fusion | flops 2106054144 | bytes 8267776 | tf_op jit(solution)/shard_map/dot_general | solution.py:88
  461.0 0.6 exponential_reduce_fusion
  461.5 0.7 broadcast_in_dim.46
  462.3 5.6 %all-to-all-start.4 = ((f32[32,3,512]{2,1,0:T(4,128)}), f32[32,3,512]{2,1,0:T(4,128)S(1)}, u32[]{:S(2)}, u32[]{:S(2)}) async-start(f32[32,3,512]{2,1,0:T(4,128)} %broadcast_in_dim.46), calls=%async_computation.6 | async-start | bytes 524288 | tf_op jit(solution)/shard_map/all_to_all | solution.py:15
  467.8 13.0 %all-to-all-done.4 = f32[32,3,512]{2,1,0:T(4,128)S(1)} async-done(((f32[32,3,512]{2,1,0:T(4,128)}), f32[32,3,512]{2,1,0:T(4,128)S(1)}, u32[]{:S(2)}, u32[]{:S(2)}) %all-to-all-start.4) | async-done | bytes 196640 | tf_op jit(solution)/shard_map/all_to_all | solution.py:15
  480.9 0.1 fusion.60
  481.7 0.1 sub.99
  481.8 0.1 reduce_sum.69
  481.9 0.7 fusion.53
  482.7 8.8 %all_to_all.43 = f32[8,1,2]{2,1,0:T(1,128)S(1)} all-to-all(f32[8,1,2]{2,1,0:T(1,128)S(1)} %broadcast_in_dim.85), channel_id=1, replica_groups=mesh['tok'=32,'cand'=8] {'cand'}, dimensions={0} | all-to-all | bytes 128 | tf_op jit(solution)/shard_map/all_to_all | solution.py:15
  491.5 0.5 reduce_max.39
  (72 shorter events, 0.9 us)
Async XLA Ops:
  8.0 18.6 %copy-start.2 = (bf16[2,128,2048]{2,1,0:T(8,128)(2,1)S(1)}, bf16[2,128,2048]{2,1,0:T(8,128)(2,1)}, u32[]{:S(2)}) copy-start(bf16[2,128,2048]{2,1,0:T(8,128)(2,1)} %param.16) | copy-start | bytes 3145732
  8.0 19.3 %copy-start.3 = (bf16[2,128,2048]{2,1,0:T(8,128)(2,1)S(1)}, bf16[2,128,2048]{2,1,0:T(8,128)(2,1)}, u32[]{:S(2)}) copy-start(bf16[2,128,2048]{2,1,0:T(8,128)(2,1)} %param.17) | copy-start | bytes 3145732
  22.6 10.2 %all-to-all-start.2 = ((bf16[8,64,256]{2,1,0:T(8,128)(2,1)}), bf16[8,64,256]{2,1,0:T(8,128)(2,1)}, u32[]{:S(2)}, u32[]{:S(2)}) async-start(bf16[8,64,256]{2,1,0:T(8,128)(2,1)} %broadcast_in_dim.42), calls=%async_computation.2 | async-start | bytes 524288 | tf_op jit(solution)/shard_map/all_to_all | solution.py:15
  29.7 16.8 %copy-start = (bf16[2,8,32,2048]{3,2,1,0:T(8,128)(2,1)S(1)}, bf16[2,8,32,2048]{3,2,1,0:T(8,128)(2,1)}, u32[]{:S(2)}) copy-start(bf16[2,8,32,2048]{3,2,1,0:T(8,128)(2,1)} %param.15) | copy-start | bytes 6291460
  32.8 65.5 %all-to-all-start = ((bf16[4,128,32,64]{1,3,0,2:T(8,128)(2,1)}), bf16[4,128,32,64]{1,3,0,2:T(8,128)(2,1)}, u32[]{:S(2)}, u32[]{:S(2)}) async-start(bf16[4,128,32,64]{1,3,0,2:T(8,128)(2,1)} %copy.67), calls=%async_computation | async-start | bytes 4194304 | tf_op jit(solution)/shard_map/all_to_all | solution.py:34
  46.4 0.7 copy-start.7
  46.4 174.8 %reduce-scatter.3.cloned.1.call-start = ((), (), s32[]{:S(2)}) async-start(), calls=%async_computation.8 | async-start | bytes 4325376 | tf_op jit(solution)/shard_map/reduce_scatter | solution.py:147
  47.1 0.7 copy-start.11
  129.0 0.9 copy-start.4
  129.0 0.9 copy-start.5
  129.0 93.2 %copy-start.8 = (f32[2048]{0:T(1024)S(1)}, f32[2048]{0:T(1024)}, u32[]{:S(2)}) copy-start(f32[2048]{0:T(1024)} %param.24) | copy-start | bytes 24580
  129.0 94.9 %copy-start.6 = (bf16[160,256]{1,0:T(8,128)(2,1)S(1)}, bf16[160,256]{1,0:T(8,128)(2,1)}, u32[]{:S(2)}) copy-start(bf16[160,256]{1,0:T(8,128)(2,1)} %param.27) | copy-start | bytes 245764
  129.1 107.3 %all-gather.7.cloned.1.call-start = ((), (), s32[]{:S(2)}) async-start(), calls=%async_computation.10 | async-start | bytes 1474560 | tf_op jit(solution)/shard_map/all_gather | solution.py:44
  130.7 148.0 %all-gather.5.cloned.1.call-start = ((), (), s32[]{:S(2)}) async-start(), calls=%async_computation.9 | async-start | bytes 2162688 | tf_op jit(solution)/shard_map/all_gather | solution.py:153
  223.9 174.5 %reduce-scatter.5.cloned.1.call-start = ((), (), s32[]{:S(2)}) async-start(), calls=%async_computation.11 | async-start | bytes 2162688 | tf_op jit(solution)/shard_map/reduce_scatter | solution.py:161
  285.9 112.5 %copy-start.1 = (f32[16,2048]{1,0:T(8,128)S(1)}, f32[16,2048]{1,0:T(8,128)}, u32[]{:S(2)}) copy-start(f32[16,2048]{1,0:T(8,128)} %reduce-scatter.3.cloned.1.call-done) | copy-start | bytes 393220
  285.9 113.5 %copy-start.10 = (f32[2048]{0:T(1024)S(1)}, f32[2048]{0:T(1024)}, u32[]{:S(2)}) copy-start(f32[2048]{0:T(1024)} %param.28) | copy-start | bytes 24580
  285.9 115.1 %copy-start.9 = (s32[2,8,32]{2,1,0:T(8,128)S(1)}, s32[2,8,32]{2,1,0:T(8,128)}, u32[]{:S(2)}) copy-start(s32[2,8,32]{2,1,0:T(8,128)} %param.20) | copy-start | bytes 6148
  285.9 115.1 %all-gather.11.cloned.1.call-start = ((), (), s32[]{:S(2)}) async-start(), calls=%async_computation.13 | async-start | bytes 4644864 | tf_op jit(solution)/shard_map/all_gather | solution.py:167
  286.5 169.3 %all-gather.9.cloned.1.call-start = ((), (), s32[]{:S(2)}) async-start(), calls=%async_computation.12 | async-start | bytes 2162688 | tf_op jit(solution)/shard_map/all_gather | solution.py:165
  460.9 21.0 %copy-start.12 = (s32[2]{0:T(128)S(1)}, s32[2]{0:T(128)}, u32[]{:S(2)}) copy-start(s32[2]{0:T(128)} %param.19) | copy-start | bytes 28
  462.3 18.6 %all-to-all-start.4 = ((f32[32,3,512]{2,1,0:T(4,128)}), f32[32,3,512]{2,1,0:T(4,128)S(1)}, u32[]{:S(2)}, u32[]{:S(2)}) async-start(f32[32,3,512]{2,1,0:T(4,128)} %broadcast_in_dim.46), calls=%async_computation.6 | async-start | bytes 524288 | tf_op jit(solution)/shard_map/all_to_all | solution.py:15
Sparse Core Ops, SparseCore 0:
  129.2 91.9 reduce-scatter.2
  286.1 112.2 reduce-scatter.4
Sparse Core Ops, SparseCore 1:
  131.3 35.1 all-gather.6
  224.0 54.6 all-gather.4
  288.1 95.5 all-gather.10
  401.1 54.7 all-gather.8
where the time goes:
time: 501 us; the launch traced here: 500 us
  waiting for transfers between devices  365 us (73%)
  matrix products  34.6 us (7%)
  blocking collectives  33.2 us (7%)
  starting transfers between devices  23.5 us (5%)
  local copies, waits for them, and re-layouts  18.3 us (4%)
  between operations  16.1 us (3%)
  other arithmetic  9.27 us (2%)
    reduce_scatter x1, waiting for transfers between devices, body(): lax.psum_scatter(ffn_terms.astype(jnp.bfloat16), 'tok', scatter_dimension...  112 us
    reduce_scatter x1, waiting for transfers between devices, body(): lax.psum_scatter(cross_terms, 'tok', scatter_dimension=0, tiled=True)  90.5 us
    all_gather x1, waiting for transfers between devices, body(): final_every = lax.all_gather(normed_final, 'tok', axis=0, tiled=True)  54.7 us
    all_to_all x1, waiting for transfers between devices, side_by_side(): lax.all_to_all(both, axis, split_axis=split_dim, concat_axis=concat_dim,...  48.7 us
    all_gather x1, waiting for transfers between devices, body(): ffn_every = lax.all_gather(normed_ffn, 'tok', axis=0, tiled=True)  42.3 us
    all_to_all x3, blocking collectives, from_everyone(): lax.all_to_all(jnp.broadcast_to(shard[None], (length, *shard.shape)), axi...  33.2 us
    all_to_all x2, waiting for transfers between devices, from_everyone(): lax.all_to_all(jnp.broadcast_to(shard[None], (length, *shard.shape)), axi...  16.1 us
    all_to_all x1, starting transfers between devices, side_by_side(): lax.all_to_all(both, axis, split_axis=split_dim, concat_axis=concat_dim,...  13.6 us
  transfers between devices with their start and end apart: 9, of which 7 were waited for; matrix products, arithmetic and copies ran while one was open for 2% of the time, Pallas kernels for 0%

commit v1 on v0

v1 whole, which is shorter than its diff:
```python
import functools

import jax
import jax.numpy as jnp
from jax import lax
from jax.experimental import pallas as pl
from jax.experimental.pallas import tpu as pltpu
from jax.sharding import PartitionSpec as P

MESH = pl.DeviceIdType.MESH
EPS = 0.25
NY, NZ, NX = 4, 4, 4
TOK, CAND = 32, 8
D = 2048
HALF = 1024
ROWS = 256
NEG = -1e30
BF = jnp.bfloat16
F32 = jnp.float32


def rms(v, gain):
    squares = jnp.mean(v * v, axis=-1, keepdims=True)
    return v * lax.rsqrt(squares + EPS) * gain


def gelu(v):
    inner = 0.7978845608028654 * (v + 0.044715 * (v * v * v))
    return 0.5 * v * (1.0 + jnp.tanh(inner))


def landed(ref, sem):
    pltpu.make_async_copy(ref, ref, sem).wait()


def kernel(
    x_in, keys, vals, lens, counts, gold, gain1, wq_in, wo_in, gain2, wi_in, fo_in, gain3, wv_in,
    scores_out, best_out,
    xv, nx, q2, kb, vb, sc, pb, at,
    wq, wo, wi, fo, wv,
    part, ryf, ryd, rya, sy, by, rzf, rzd, rza, sz, ac, nf,
    hid, st, f1, f2,
    kv_recv, kv_send, g_recv, g_send, g_own, g_dual, g_dsend,
    rs_recv, rs_send, ag_recv, ag_send, f_recv, f_send, l_sem,
):
    t = lax.axis_index("tok")
    c = lax.axis_index("cand")
    k = lax.rem(t, 2)
    j = lax.div(t, 2)
    y = lax.div(j, NZ)
    z = lax.rem(j, NZ)
    xx = lax.div(c, 2)
    zl = lax.rem(c, 2)

    def tok_of(yy, zz):
        return (lax.rem(yy, NY) * NZ + lax.rem(zz, NZ)) * 2 + k

    def cand_of(x_at, z_at):
        return lax.rem(x_at, NX) * 2 + z_at

    partner = t + 1 - 2 * k
    cz = cand_of(xx, 1 - zl)
    cp, cm = cand_of(xx + 1, zl), cand_of(xx + 3, zl)
    cpz, cmz = cand_of(xx + 1, 1 - zl), cand_of(xx + 3, 1 - zl)
    co, coz = cand_of(xx + 2, zl), cand_of(xx + 2, 1 - zl)

    def send(src, dst, s_sem, r_sem, tok, cand):
        pltpu.make_async_remote_copy(
            src_ref=src, dst_ref=dst, send_sem=s_sem, recv_sem=r_sem,
            device_id=(tok, cand), device_id_type=MESH,
        ).start()

    x_copy = pltpu.make_async_copy(x_in.at[k], xv, l_sem.at[0])
    x_copy.start()

    barrier = pltpu.get_barrier_semaphore()

    @pl.loop(1, TOK)
    def _(d):
        pl.semaphore_signal(
            barrier, inc=1, device_id=(lax.rem(t + d, TOK), c), device_id_type=MESH
        )

    @pl.loop(1, CAND)
    def _(d):
        pl.semaphore_signal(
            barrier, inc=1, device_id=(t, lax.rem(c + d, CAND)), device_id_type=MESH
        )
        pl.semaphore_signal(
            barrier, inc=1, device_id=(partner, lax.rem(c + d, CAND)), device_id_type=MESH
        )

    def q_at(cc, part=None):
        if part is None:
            return wq.at[k, pl.ds(256 * cc, 256), :]
        return wq.at[k, pl.ds(256 * cc + 128 * part, 128), :]

    def o_at(cc, part=None):
        if part is None:
            return wo.at[cc, pl.ds(64 * k, 64), :]
        return wo.at[cc, pl.ds(64 * k + 32 * part, 32), :]

    def i_at(cc, part=None):
        if part is None:
            return wi.at[k, pl.ds(256 * cc, 256), :]
        return wi.at[k, pl.ds(256 * cc + 128 * part, 128), :]

    def fo_at(cc, part=None):
        if part is None:
            return fo.at[cc, pl.ds(160 * k, 160), :]
        return fo.at[cc, pl.ds(160 * k + 80 * part, 80), :]

    def v_at(cc, part=None):
        if part is None:
            return wv.at[k, pl.ds(256 * cc, 256), :]
        return wv.at[k, pl.ds(256 * cc + 128 * part, 128), :]

    def kv_at(ref):
        def at_(cc, part=None):
            if part is None:
                return ref.at[pl.ds(512 * cc, 512), :]
            return ref.at[pl.ds(512 * cc + 256 * part, 256), :]
        return at_

    places = [q_at, o_at, i_at, fo_at, v_at, kv_at(kb), kv_at(vb)]
    whole = [
        lambda h: wq.at[h], lambda h: wo.at[:, pl.ds(64 * h, 64), :], lambda h: wi.at[h],
        lambda h: fo.at[:, pl.ds(160 * h, 160), :], lambda h: wv.at[h],
    ]
    inputs = [wq_in, wo_in, wi_in, fo_in, wv_in]

    def own_copy(n):
        return pltpu.make_async_copy(inputs[n], places[n](c), g_own.at[n])

    def g_send_to(n, slot, src, dst, cand):
        send(src, dst, g_send.at[n, slot], g_recv.at[n, slot], t, cand)

    def step1(n):
        at_, src = places[n], (inputs[n] if n < 5 else places[n](c))
        g_send_to(n, 0, src, at_(c), cz)
        g_send_to(n, 1, src, at_(c), cp)
        g_send_to(n, 2, src, at_(c), cm)

    def step2(n):
        at_ = places[n]
        landed(at_(cz), g_recv.at[n, 0])
        g_send_to(n, 3, at_(cz), at_(cz), cp)
        g_send_to(n, 4, at_(cz), at_(cz), cm)
        landed(at_(cm), g_recv.at[n, 1])
        g_send_to(n, 5, at_(cm, 0), at_(cm, 0), cp)
        landed(at_(cp), g_recv.at[n, 2])
        g_send_to(n, 6, at_(cp, 1), at_(cp, 1), cm)

    def step3(n):
        at_ = places[n]
        landed(at_(cmz), g_recv.at[n, 3])
        g_send_to(n, 7, at_(cmz, 0), at_(cmz, 0), cp)
        landed(at_(cpz), g_recv.at[n, 4])
        g_send_to(n, 8, at_(cpz, 1), at_(cpz, 1), cm)

    def step4(n):
        at_ = places[n]
        landed(at_(co, 0), g_recv.at[n, 5])
        landed(at_(co, 1), g_recv.at[n, 6])
        landed(at_(coz, 0), g_recv.at[n, 7])
        landed(at_(coz, 1), g_recv.at[n, 8])
        if n < 5:
            own_copy(n).wait()
            send(whole[n](k), whole[n](k), g_dsend.at[n], g_dual.at[n], partner, c)

    def both(n):
        landed(whole[n](1 - k), g_dual.at[n])

    for n in range(5):
        own_copy(n).start()

    x_copy.wait()

    @pl.loop(0, 8)
    def _(i):
        rows = xv[i].astype(F32)
        nx[pl.ds(pl.multiple_of(32 * i, 32), 32), :] = rms(rows, gain1[...]).astype(BF)

    pl.semaphore_wait(barrier, TOK - 1 + 2 * (CAND - 1))

    step1(0)

    for n, (src, dst) in enumerate(((keys, kb), (vals, vb))):
        here = dst.at[pl.ds(512 * c + 16 * t, 16), :]
        pltpu.make_async_copy(
            src.at[k, pl.ds(16 * c, 16), pl.ds(pl.multiple_of(128 * j, 128), 128)],
            here, l_sem.at[1 + n],
        ).start()

        @pl.loop(1, TOK)
        def _(d, src=src, n=n, here=here):
            to = lax.rem(t + d, TOK)
            send(
                src.at[
                    lax.rem(to, 2), pl.ds(16 * c, 16),
                    pl.ds(pl.multiple_of(128 * lax.div(to, 2), 128), 128),
                ],
                here, kv_send.at[n], kv_recv.at[n], to, c,
            )

    def kv_mine(n):
        ref = (kb, vb)[n]
        pltpu.make_async_copy(
            ref.at[pl.ds(0, 16), :], ref.at[pl.ds(512 * c + 16 * t, 16), :], l_sem.at[1 + n]
        ).wait()
        landed(ref.at[pl.ds(0, 496), :], kv_recv.at[n])

    step1(1)
    step1(2)
    step1(3)

    step2(0)
    step3(0)
    step4(0)
    kv_mine(0)
    step1(5)
    kv_mine(1)
    step1(6)
    both(0)
    zero = jnp.zeros((ROWS, 64), BF)
    first = jnp.dot(nx[...], wq[0], preferred_element_type=F32).astype(BF)
    q2[pl.ds(0, ROWS), :] = jnp.concatenate([first, zero], axis=1)
    second = jnp.dot(nx[...], wq[1], preferred_element_type=F32).astype(BF)
    q2[pl.ds(ROWS, ROWS), :] = jnp.concatenate([zero, second], axis=1)

    length = lens[k]

    def score(cc):
        place = lax.broadcasted_iota(jnp.int32, (1, 512), 1)
        token = lax.div(place, 16) * 128 + 16 * cc + lax.rem(place, 16)
        live = token < length
        block = kb[pl.ds(pl.multiple_of(512 * cc, 512), 512), :]

        @pl.loop(0, 4)
        def _(r):
            rows = pl.ds(pl.multiple_of(128 * r, 128), 128)
            s = lax.dot_general(
                q2[rows, :], block, (((1,), (1,)), ((), ())), preferred_element_type=F32
            )
            sc[cc, rows, :] = jnp.where(live, s, NEG)

    step2(5)
    step2(6)
    score(c)
    step3(5)
    step3(6)
    step1(4)
    score(cz)
    score(cm)
    score(cp)
    step2(1)
    step2(2)
    step2(3)
    score(cmz)
    score(cpz)
    step4(5)
    score(co)
    score(coz)
    step3(1)
    step3(2)
    step3(3)

    @pl.loop(0, 16)
    def _(r):
        rows = pl.ds(pl.multiple_of(32 * r, 32), 32)
        high = sc[0, rows, :]
        for cc in range(1, CAND):
            high = jnp.maximum(high, sc[cc, rows, :])
        top = jnp.max(high, axis=1, keepdims=True)
        total = jnp.zeros((32, 512), F32)
        for cc in range(CAND):
            w = jnp.exp(sc[cc, rows, :] - top)
            total = total + w
            pb[rows, pl.ds(512 * cc, 512)] = w.astype(BF)
        st[rows, :] = jnp.broadcast_to(jnp.sum(total, axis=1, keepdims=True), (32, 128))

    step4(1)
    step4(2)
    step4(3)
    step4(6)

    @pl.loop(0, 4)
    def _(r):
        low = pl.ds(pl.multiple_of(64 * r, 64), 64)
        upp = pl.ds(pl.multiple_of(64 * r + ROWS, 64), 64)
        a = jnp.dot(pb[low, :], vb[...], preferred_element_type=F32) / st[low, :]
        b = jnp.dot(pb[upp, :], vb[...], preferred_element_type=F32) / st[upp, :]
        lane = lax.broadcasted_iota(jnp.int32, (64, 128), 1)
        at[low, :] = jnp.where(lane < 64, a, b).astype(BF)

    both(1)
    for cc in range(CAND):
        part[0, cc // 4, :, pl.ds(256 * (cc % 4), 256)] = jnp.dot(
            at[...], wo[cc], preferred_element_type=F32
        ).astype(BF)

    ty, tm = tok_of(y + 1, z), tok_of(y + 3, z)
    tz, tn = tok_of(y, z + 1), tok_of(y, z + 3)

    def y_rows(dy):
        return pl.ds(pl.multiple_of(64 * lax.rem(y + dy, NY), 64), 64)

    def z_rows(dz):
        return pl.ds(pl.multiple_of(16 * lax.rem(z + dz, NZ), 16), 16)

    my_rows = pl.ds(pl.multiple_of(64 * y + 16 * z, 16), 16)

    def reduce_sums(p):
        def go(n, src, dst, tok):
            send(src, dst, rs_send.at[p, n], rs_recv.at[p, n], tok, c)

        go(0, part.at[p, 0, y_rows(2)], ryf.at[p, 0], ty)
        go(1, part.at[p, 1, y_rows(2)], ryf.at[p, 1], tm)
        go(2, part.at[p, 1, y_rows(1)], ryd.at[p, 1], ty)
        go(3, part.at[p, 0, y_rows(3)], ryd.at[p, 0], tm)
        landed(ryf.at[p, 0], rs_recv.at[p, 0])
        sy[p, 0] = (ryf[p, 0].astype(F32) + part[p, 0, y_rows(1)].astype(F32)).astype(BF)
        go(4, sy.at[p, 0], rya.at[p, 0], ty)
        landed(ryf.at[p, 1], rs_recv.at[p, 1])
        sy[p, 1] = (ryf[p, 1].astype(F32) + part[p, 1, y_rows(3)].astype(F32)).astype(BF)
        go(5, sy.at[p, 1], rya.at[p, 1], tm)
        landed(ryd.at[p, 1], rs_recv.at[p, 2])
        landed(ryd.at[p, 0], rs_recv.at[p, 3])
        for h in range(2):
            landed(rya.at[p, h], rs_recv.at[p, 4 + h])
            by[p, h] = (
                rya[p, h].astype(F32) + ryd[p, h].astype(F32)
                + part[p, h, y_rows(0)].astype(F32)
            ).astype(BF)
        go(6, by.at[p, 0, z_rows(2)], rzf.at[p, 0], tz)
        go(7, by.at[p, 1, z_rows(2)], rzf.at[p, 1], tn)
        go(8, by.at[p, 1, z_rows(1)], rzd.at[p, 1], tz)
        go(9, by.at[p, 0, z_rows(3)], rzd.at[p, 0], tn)
        landed(rzf.at[p, 0], rs_recv.at[p, 6])
        sz[p, 0] = (rzf[p, 0].astype(F32) + by[p, 0, z_rows(1)].astype(F32)).astype(BF)
        go(10, sz.at[p, 0], rza.at[p, 0], tz)
        landed(rzf.at[p, 1], rs_recv.at[p, 7])
        sz[p, 1] = (rzf[p, 1].astype(F32) + by[p, 1, z_rows(3)].astype(F32)).astype(BF)
        go(11, sz.at[p, 1], rza.at[p, 1], tn)
        landed(rzd.at[p, 1], rs_recv.at[p, 8])
        landed(rzd.at[p, 0], rs_recv.at[p, 9])
        sums = []
        for h in range(2):
            landed(rza.at[p, h], rs_recv.at[p, 10 + h])
            sums.append(
                rza[p, h].astype(F32) + rzd[p, h].astype(F32)
                + by[p, h, z_rows(0)].astype(F32)
            )
        return jnp.concatenate(sums, axis=1)

    def spread(p, value):
        nf[p, 0, my_rows, :] = value[:, :HALF]
        nf[p, 1, my_rows, :] = value[:, HALF:]

        def go(n, where, tok):
            send(where, where, ag_send.at[p, n], ag_recv.at[p, n], tok, c)

        def z_block(dz):
            return pl.ds(pl.multiple_of(64 * y + 16 * lax.rem(z + dz, NZ), 16), 16)

        go(0, nf.at[p, :, my_rows, :], tz)
        go(1, nf.at[p, :, my_rows, :], tn)
        landed(nf.at[p, :, z_block(3), :], ag_recv.at[p, 0])
        go(2, nf.at[p, 0, z_block(3), :], tz)
        landed(nf.at[p, :, z_block(1), :], ag_recv.at[p, 1])
        go(3, nf.at[p, 1, z_block(1), :], tn)
        landed(nf.at[p, 0, z_block(2), :], ag_recv.at[p, 2])
        landed(nf.at[p, 1, z_block(2), :], ag_recv.at[p, 3])
        go(4, nf.at[p, :, y_rows(0), :], ty)
        go(5, nf.at[p, :, y_rows(0), :], tm)
        landed(nf.at[p, :, y_rows(3), :], ag_recv.at[p, 4])
        go(6, nf.at[p, 0, y_rows(3), :], ty)
        landed(nf.at[p, :, y_rows(1), :], ag_recv.at[p, 5])
        go(7, nf.at[p, 1, y_rows(1), :], tm)
        landed(nf.at[p, 0, y_rows(2), :], ag_recv.at[p, 6])
        landed(nf.at[p, 1, y_rows(2), :], ag_recv.at[p, 7])

    mine = xv[2 * y + lax.div(z, 2), pl.ds(pl.multiple_of(16 * lax.rem(z, 2), 16), 16), :]
    ac[...] = mine.astype(F32) + reduce_sums(0)
    step2(4)
    spread(0, rms(ac[...], gain2[...]).astype(BF))
    step3(4)
    both(2)
    both(3)

    @pl.loop(0, 4)
    def _(r):
        rows = pl.ds(pl.multiple_of(64 * r, 64), 64)
        for h in range(2):
            o = jnp.dot(
                nf[0, 0, rows, :], wi[h, pl.ds(0, HALF), :], preferred_element_type=F32
            ) + jnp.dot(
                nf[0, 1, rows, :], wi[h, pl.ds(HALF, HALF), :], preferred_element_type=F32
            )
            hid[h, rows, :] = (gelu(o[:, :160]) * o[:, 160:320]).astype(BF)
        for cc in range(CAND):
            part[1, cc // 4, rows, pl.ds(256 * (cc % 4), 256)] = (
                jnp.dot(hid[0, rows, :], fo[cc, pl.ds(0, 160), :], preferred_element_type=F32)
                + jnp.dot(hid[1, rows, :], fo[cc, pl.ds(160, 160), :], preferred_element_type=F32)
            ).astype(BF)

    after = ac[...] + reduce_sums(1)
    step4(4)
    spread(1, rms(after, gain3[...]).astype(BF))
    both(4)

    width = wv.shape[2]
    ids = gold[k].astype(F32)
    eye = lax.broadcasted_iota(jnp.int32, (32, 32), 0) == lax.broadcasted_iota(jnp.int32, (32, 32), 1)
    start = [((2 * j + h) * width).astype(F32) for h in range(2)]

    for i in range(8):
        column = jnp.sum(
            jnp.where(eye, jnp.broadcast_to(ids[i : i + 1, :], (32, 32)), 0.0), axis=1, keepdims=True
        )
        st[pl.ds(32 * i, 32), :] = jnp.broadcast_to(column, (32, 128))

    @pl.loop(0, 4)
    def _(r):
        rows = pl.ds(pl.multiple_of(64 * r, 64), 64)
        wanted = st[rows, :][:, :1]
        logits = []
        for h in range(2):
            logits.append(
                jnp.dot(nf[1, 0, rows, :], wv[h, pl.ds(0, HALF), :], preferred_element_type=F32)
                + jnp.dot(nf[1, 1, rows, :], wv[h, pl.ds(HALF, HALF), :], preferred_element_type=F32)
            )
        high = jnp.maximum(
            jnp.max(logits[0], axis=1, keepdims=True), jnp.max(logits[1], axis=1, keepdims=True)
        )
        total = jnp.zeros((64, 1), F32)
        picked = jnp.zeros((64, 1), F32)
        for h in range(2):
            total = total + jnp.sum(jnp.exp(logits[h] - high), axis=1, keepdims=True)
            at_col = lax.broadcasted_iota(jnp.int32, (64, width), 1).astype(F32) + start[h]
            picked = picked + jnp.sum(
                jnp.where(at_col == wanted, logits[h], 0.0), axis=1, keepdims=True
            )
        lane = lax.broadcasted_iota(jnp.int32, (64, 128), 1)
        st[pl.ds(pl.multiple_of(256 + 64 * r, 64), 64), :] = jnp.where(
            lane == 0, high, jnp.where(lane == 1, total, picked)
        )

    stats = st[pl.ds(256, 256), :].T
    f1[j] = stats[0:8, :]

    @pl.loop(1, 16)
    def _(d):
        to = lax.rem(j + d, 16) * 2 + k
        send(f1.at[j], f1.at[j], f_send.at[0], f_recv.at[0], to, c)

    landed(f1.at[pl.ds(0, 15)], f_recv.at[0])
    top = f1[0][0:1, :]
    for n in range(1, 16):
        top = jnp.maximum(top, f1[n][0:1, :])
    total = jnp.zeros((1, ROWS), F32)
    picked = jnp.zeros((1, ROWS), F32)
    for n in range(16):
        total = total + f1[n][1:2, :] * jnp.exp(f1[n][0:1, :] - top)
        picked = picked + f1[n][2:3, :]
    logprob = picked - top - jnp.log(total)
    group = lax.div(lax.broadcasted_iota(jnp.int32, (8, ROWS), 1), 32)
    whose = lax.broadcasted_iota(jnp.int32, (8, ROWS), 0)
    per = jnp.sum(jnp.where(group == whose, logprob, 0.0), axis=1, keepdims=True) * (1.0 / 32)
    diag = lax.broadcasted_iota(jnp.int32, (8, 128), 0) == lax.broadcasted_iota(jnp.int32, (8, 128), 1)
    row = jnp.sum(jnp.where(diag, per, 0.0), axis=0, keepdims=True)
    f2[8 * k + c] = jnp.broadcast_to(row, (8, 128))

    @pl.loop(1, CAND)
    def _(d):
        to = lax.rem(c + d, CAND)
        send(f2.at[8 * k + c], f2.at[8 * k + c], f_send.at[1], f_recv.at[1], t, to)
        send(f2.at[8 * k + c], f2.at[8 * k + c], f_send.at[1], f_recv.at[1], partner, to)

    send(f2.at[8 * k + c], f2.at[8 * k + c], f_send.at[1], f_recv.at[1], partner, c)
    landed(f2.at[pl.ds(0, 15)], f_recv.at[1])
    lane = lax.broadcasted_iota(jnp.int32, (8, 8, 128), 2)
    cand = lax.broadcasted_iota(jnp.int32, (8, 8, 128), 0) * 8 + lane
    for b in range(2):
        count = counts[b]
        inside = jnp.where((cand < count) & (lane < 8), f2[pl.ds(8 * b, 8)], NEG)
        best_out[b] = jnp.max(inside)
        own_lane = lax.broadcasted_iota(jnp.int32, (1, 128), 1)
        own = f2[8 * b + c][0:1, :]
        scores_out[pl.ds(b, 1), :] = jnp.where(own_lane + 8 * c < count, own, 0.0)[:, :8]

    for n in range(2):
        landed(kb.at[pl.ds(0, 496), :], kv_send.at[n])
    for n in range(7):
        at_ = places[n]
        for slot in range(9):
            landed(at_(c) if slot < 5 else at_(c, 0), g_send.at[n, slot])
        if n < 5:
            landed(whole[n](k), g_dsend.at[n])
    for p in range(2):
        for n in range(6):
            landed(sy.at[p, 0], rs_send.at[p, n])
            landed(sz.at[p, 0], rs_send.at[p, 6 + n])
        for n, ref in enumerate(
            [nf.at[p, :, my_rows, :]] * 2 + [nf.at[p, 0, my_rows, :]] * 2
            + [nf.at[p, :, y_rows(0), :]] * 2 + [nf.at[p, 0, y_rows(0), :]] * 2
        ):
            landed(ref, ag_send.at[p, n])
    landed(f1.at[pl.ds(0, 15)], f_send.at[0])
    landed(f2.at[pl.ds(0, 15)], f_send.at[1])


def body(
    dec_hidden, enc_keys, enc_values, enc_lengths, cand_counts, gold_ids, gain_cross, w_query,
    w_out, gain_ffn, w_in_gate, w_in_up, w_ffn_out, gain_final, w_vocab,
):
    units = w_in_gate.shape[1]
    width = w_vocab.shape[1]
    w_in = jnp.concatenate([w_in_gate, w_in_up], axis=1)
    anywhere = pl.BlockSpec(memory_space=pl.ANY)
    vmem = pl.BlockSpec(memory_space=pltpu.VMEM)
    smem = pl.BlockSpec(memory_space=pltpu.SMEM)
    dma = pltpu.SemaphoreType.DMA
    return pl.pallas_call(
        kernel,
        name="layer",
        out_shape=(
            jax.ShapeDtypeStruct((2, 8), F32),
            jax.ShapeDtypeStruct((2,), F32),
        ),
        in_specs=[
            anywhere, anywhere, anywhere, smem, smem, vmem, vmem, anywhere, anywhere, vmem,
            anywhere, anywhere, vmem, anywhere,
        ],
        out_specs=(vmem, smem),
        scratch_shapes=[
            pltpu.VMEM((8, 32, D), BF),
            pltpu.VMEM((ROWS, D), BF),
            pltpu.VMEM((2 * ROWS, 128), BF),
            pltpu.VMEM((4096, 128), BF),
            pltpu.VMEM((4096, 128), BF),
            pltpu.VMEM((8, 2 * ROWS, 512), F32),
            pltpu.VMEM((2 * ROWS, 4096), BF),
            pltpu.VMEM((ROWS, 128), BF),
            pltpu.VMEM((2, D, 64), BF),
            pltpu.VMEM((8, 128, 256), BF),
            pltpu.VMEM((2, D, 2 * units), BF),
            pltpu.VMEM((8, 2 * units, 256), BF),
            pltpu.VMEM((2, D, width), BF),
            pltpu.VMEM((2, 2, ROWS, HALF), BF),
            pltpu.VMEM((2, 2, 64, HALF), BF),
            pltpu.VMEM((2, 2, 64, HALF), BF),
            pltpu.VMEM((2, 2, 64, HALF), BF),
            pltpu.VMEM((2, 2, 64, HALF), BF),
            pltpu.VMEM((2, 2, 64, HALF), BF),
            pltpu.VMEM((2, 2, 16, HALF), BF),
            pltpu.VMEM((2, 2, 16, HALF), BF),
            pltpu.VMEM((2, 2, 16, HALF), BF),
            pltpu.VMEM((2, 2, 16, HALF), BF),
            pltpu.VMEM((16, D), F32),
            pltpu.VMEM((2, 2, ROWS, HALF), BF),
            pltpu.VMEM((2, ROWS, units), BF),
            pltpu.VMEM((2 * ROWS, 128), F32),
            pltpu.VMEM((16, 8, ROWS), F32),
            pltpu.VMEM((16, 8, 128), F32),
            dma((2,)), dma((2,)), dma((7, 9)), dma((7, 9)), dma((5,)), dma((5,)), dma((5,)),
            dma((2, 12)), dma((2, 12)), dma((2, 8)), dma((2, 8)), dma((2,)), dma((2,)), dma((3,)),
        ],
        compiler_params=pltpu.CompilerParams(
            collective_id=0, has_side_effects=True, vmem_limit_bytes=62 * 1024 * 1024
        ),
    )(
        dec_hidden, enc_keys, enc_values, enc_lengths, cand_counts, gold_ids,
        gain_cross.reshape(1, -1), w_query, w_out, gain_ffn.reshape(1, -1), w_in, w_ffn_out,
        gain_final.reshape(1, -1), w_vocab,
    )


def solution(mesh):
    in_specs = (
        P(None, "cand", None, None), P(None, "tok", None), P(None, "tok", None), P(), P(),
        P(None, "cand", None), P(), P("cand", "tok"), P("tok", "cand"), P(), P("cand", "tok"),
        P("cand", "tok"), P("tok", "cand"), P(), P("cand", "tok"),
    )
    return jax.shard_map(
        body, mesh=mesh, in_specs=in_specs, out_specs=(P(None, "cand"), P()), check_vma=False
    )
```

time: 501 us -> 184 us (0.37)
  waiting for transfers between devices: 365 us -> 0 us
  Pallas kernels: 0 us -> 175 us
  matrix products: 34.6 us -> 0 us
  blocking collectives: 33.2 us -> 0 us
  starting transfers between devices: 23.5 us -> 0 us
  between operations: 16.1 us -> 0.65 us
  local copies, waits for them, and re-layouts: 18.3 us -> 7.84 us
  other arithmetic: 9.27 us -> 0.78 us
    reduce_scatter x2 -> x0, waiting for transfers between devices: 202 us -> none  [the longest x1 112 us: body(): lax.psum_scatter(ffn_terms.astype(jnp.bfloat16), 'tok', scatter_dimension...]
    pallas_call x0 -> x1, Pallas kernels: none -> 175 us  [body(): pl.pallas_call(kernel, name='layer', out_shape=(jax.ShapeDtypeStruct((2,...]
    all_gather x4 -> x0, waiting for transfers between devices: 97 us -> none  [the longest x1 54.7 us: body(): final_every = lax.all_gather(normed_final, 'tok', axis=0, tiled=True)]
    all_to_all x3 -> x0, waiting for transfers between devices: 64.8 us -> none  [the longest x1 48.7 us: side_by_side(): lax.all_to_all(both, axis, split_axis=split_dim, concat_axis=concat_dim,...]
    all_to_all x3 -> x0, blocking collectives: 33.2 us -> none  [from_everyone(): lax.all_to_all(jnp.broadcast_to(shard[None], (length, *shard.shape)), axi...]
    dot_general x7 -> x0, matrix products: 31 us -> none  [the longest x1 10.6 us: body(): jnp.einsum('bhrs,bshd->brhd', weights.astype(jnp.bfloat16), values_heads,...]
    all_to_all x3 -> x0, starting transfers between devices: 23.2 us -> none  [the longest x1 13.6 us: side_by_side(): lax.all_to_all(both, axis, split_axis=split_dim, concat_axis=concat_dim,...]
    split x3 -> x0, local copies, waits for them, and re-layouts: 6.39 us -> none  [side_by_side(): jnp.split(result, [sum(widths[:k]) for k in range(1, len(widths))], axis=...]
  transfers between devices with their start and end apart: 9 -> 0, of which waited for: 7 -> 0; matrix products, arithmetic and copies ran while one was open for 2% -> 0% of each run, Pallas kernels for 0% -> 0%
where the time goes in v1:
time: 184 us
  Pallas kernels  175 us (95%)
  local copies, waits for them, and re-layouts  7.84 us (4%)
    pallas_call x1, Pallas kernels, body(): pl.pallas_call(kernel, name='layer', out_shape=(jax.ShapeDtypeStruct((2,...  175 us
    unnamed x6, local copies, waits for them, and re-layouts  7.84 us

profile of v1, /device:TPU:1, one launch (start us, length us, event | category | flops | bytes accessed | tf_op | source)
XLA Modules:
  0.0 184.1 jit_solution(14843617341640229002)
XLA Ops:
  0.6 1.5 copy.19.wq_in
  2.1 1.0 copy.17
  3.1 1.0 copy.18
  4.1 0.8 pad_maximum_fusion.wi_in
  4.9 2.0 %copy.20.wv_in = bf16[256,1004]{1,0:T(8,128)(2,1)} copy(bf16[256,1004]{0,1:T(8,128)(2,1)} %param.29) | data formatting | bytes 1028096 | tf_op args[14]
  6.9 174.8 %layer.1 = (f32[2,8]{1,0:T(2,128)}, f32[2]{0:T(128)}) custom-call(bf16[2,8,32,2048]{3,2,1,0:T(8,128)(2,1)} %x_in.1, bf16[2,128,2048]{2,1,0:T(8,128)(2,1)} %keys.1, bf16[2,128,2048]{2,1,0:T(8,128)(2,1)} %vals.1, s32[2]{0:T(128)} %lens.1, s32[2]{0:T(128)} %counts.1, s32[2,8,32]{2,1,0:T(8,128)} %gold.1, f32[1,2048]{1,0:T(1,128)} %bitcast.3, ...), custom_call_target="tpu_custom_call" | custom-call | tf_op jit(solution)/shard_map/layer/pallas_call | solution.py:524
  181.8 1.2 copy.23
  183.0 1.1 copy.24

commit v2 on v1

--- a/solution.py
+++ b/solution.py
@@ -29,12 +29,16 @@
     return 0.5 * v * (1.0 + jnp.tanh(inner))
 
 
+def dot_t(a, b):
+    return lax.dot_general(a, b, (((1,), (1,)), ((), ())), preferred_element_type=F32)
+
+
 def landed(ref, sem):
     pltpu.make_async_copy(ref, ref, sem).wait()
 
 
 def kernel(
-    x_in, keys, vals, lens, counts, gold, gain1, wq_in, wo_in, gain2, wi_in, fo_in, gain3, wv_in,
+    x_in, keys, vals, lens, counts, gold, gain1, wq_in, wo_in, gain2, wg_in, wu_in, fo_in, gain3, wv_in,
     scores_out, best_out,
     xv, nx, q2, kb, vb, sc, pb, at,
     wq, wo, wi, fo, wv,
@@ -90,30 +94,24 @@
             barrier, inc=1, device_id=(partner, lax.rem(c + d, CAND)), device_id_type=MESH
         )
 
-    def q_at(cc, part=None):
-        if part is None:
-            return wq.at[k, pl.ds(256 * cc, 256), :]
-        return wq.at[k, pl.ds(256 * cc + 128 * part, 128), :]
-
-    def o_at(cc, part=None):
-        if part is None:
-            return wo.at[cc, pl.ds(64 * k, 64), :]
-        return wo.at[cc, pl.ds(64 * k + 32 * part, 32), :]
+    def stacked(ref, size):
+        def at_(cc, part=None):
+            if part is None:
+                return ref.at[cc, pl.ds(size * k, size), :]
+            return ref.at[cc, pl.ds(size * k + size // 2 * part, size // 2), :]
+        return at_
 
     def i_at(cc, part=None):
         if part is None:
-            return wi.at[k, pl.ds(256 * cc, 256), :]
-        return wi.at[k, pl.ds(256 * cc + 128 * part, 128), :]
-
-    def fo_at(cc, part=None):
-        if part is None:
-            return fo.at[cc, pl.ds(160 * k, 160), :]
-        return fo.at[cc, pl.ds(160 * k + 80 * part, 80), :]
+            return wi.at[:, cc, pl.ds(160 * k, 160), :]
+        return wi.at[:, cc, pl.ds(160 * k + 80 * part, 80), :]
+
+    width = wv.shape[2]
 
     def v_at(cc, part=None):
         if part is None:
-            return wv.at[k, pl.ds(256 * cc, 256), :]
-        return wv.at[k, pl.ds(256 * cc + 128 * part, 128), :]
+            return wv.at[k, cc]
+        return wv.at[k, cc, pl.ds(0, 512), :] if part == 0 else wv.at[k, cc, pl.ds(512, width - 512), :]
 
     def kv_at(ref):
         def at_(cc, part=None):
@@ -122,21 +120,29 @@
             return ref.at[pl.ds(512 * cc + 256 * part, 256), :]
         return at_
 
-    places = [q_at, o_at, i_at, fo_at, v_at, kv_at(kb), kv_at(vb)]
+    places = [stacked(wq, 64), stacked(wo, 64), i_at, stacked(fo, 160), v_at, kv_at(kb), kv_at(vb)]
     whole = [
-        lambda h: wq.at[h], lambda h: wo.at[:, pl.ds(64 * h, 64), :], lambda h: wi.at[h],
-        lambda h: fo.at[:, pl.ds(160 * h, 160), :], lambda h: wv.at[h],
+        lambda h: wq.at[:, pl.ds(64 * h, 64), :], lambda h: wo.at[:, pl.ds(64 * h, 64), :],
+        lambda h: wi.at[:, :, pl.ds(160 * h, 160), :], lambda h: fo.at[:, pl.ds(160 * h, 160), :],
+        lambda h: wv.at[h],
     ]
-    inputs = [wq_in, wo_in, wi_in, fo_in, wv_in]
-
-    def own_copy(n):
-        return pltpu.make_async_copy(inputs[n], places[n](c), g_own.at[n])
+
+    def own_copies():
+        for n, src in ((0, wq_in), (1, wo_in), (3, fo_in), (4, wv_in)):
+            pltpu.make_async_copy(src, places[n](c), g_own.at[n]).start()
+        for m, src in enumerate((wg_in, wu_in)):
+            pltpu.make_async_copy(
+                src, wi.at[m, c, pl.ds(160 * k, 160), :], g_own.at[2]
+            ).start()
 
     def g_send_to(n, slot, src, dst, cand):
         send(src, dst, g_send.at[n, slot], g_recv.at[n, slot], t, cand)
 
     def step1(n):
-        at_, src = places[n], (inputs[n] if n < 5 else places[n](c))
+        at_ = places[n]
+        src = at_(c)
+        if n < 5:
+            landed(src, g_own.at[n])
         g_send_to(n, 0, src, at_(c), cz)
         g_send_to(n, 1, src, at_(c), cp)
         g_send_to(n, 2, src, at_(c), cm)
@@ -165,14 +171,13 @@
         landed(at_(coz, 0), g_recv.at[n, 7])
         landed(at_(coz, 1), g_recv.at[n, 8])
         if n < 5:
-            own_copy(n).wait()
             send(whole[n](k), whole[n](k), g_dsend.at[n], g_dual.at[n], partner, c)
 
     def both(n):
         landed(whole[n](1 - k), g_dual.at[n])
 
-    for n in range(5):
-        own_copy(n).start()
+
+    own_copies()
 
     x_copy.wait()
 
@@ -210,12 +215,11 @@
         ).wait()
         landed(ref.at[pl.ds(0, 496), :], kv_recv.at[n])
 
+    step2(0)
+    step1(3)
+    step3(0)
     step1(1)
     step1(2)
-    step1(3)
-
-    step2(0)
-    step3(0)
     step4(0)
     kv_mine(0)
     step1(5)
@@ -223,10 +227,12 @@
     step1(6)
     both(0)
     zero = jnp.zeros((ROWS, 64), BF)
-    first = jnp.dot(nx[...], wq[0], preferred_element_type=F32).astype(BF)
-    q2[pl.ds(0, ROWS), :] = jnp.concatenate([first, zero], axis=1)
-    second = jnp.dot(nx[...], wq[1], preferred_element_type=F32).astype(BF)
-    q2[pl.ds(ROWS, ROWS), :] = jnp.concatenate([zero, second], axis=1)
+    query = jnp.zeros((ROWS, 128), F32)
+    for cc in range(CAND):
+        query = query + dot_t(nx[:, 256 * cc : 256 * cc + 256], wq[cc])
+    query = query.astype(BF)
+    q2[pl.ds(0, ROWS), :] = jnp.concatenate([query[:, :64], zero], axis=1)
+    q2[pl.ds(ROWS, ROWS), :] = jnp.concatenate([zero, query[:, 64:]], axis=1)
 
     length = lens[k]
 
@@ -239,31 +245,25 @@
         @pl.loop(0, 4)
         def _(r):
             rows = pl.ds(pl.multiple_of(128 * r, 128), 128)
-            s = lax.dot_general(
-                q2[rows, :], block, (((1,), (1,)), ((), ())), preferred_element_type=F32
-            )
+            s = dot_t(q2[rows, :], block)
             sc[cc, rows, :] = jnp.where(live, s, NEG)
 
     step2(5)
     step2(6)
     score(c)
     step3(5)
-    step3(6)
-    step1(4)
     score(cz)
     score(cm)
-    score(cp)
+    step3(6)
     step2(1)
     step2(2)
     step2(3)
+    score(cp)
     score(cmz)
     score(cpz)
     step4(5)
     score(co)
     score(coz)
-    step3(1)
-    step3(2)
-    step3(3)
 
     @pl.loop(0, 16)
     def _(r):
@@ -279,9 +279,7 @@
             pb[rows, pl.ds(512 * cc, 512)] = w.astype(BF)
         st[rows, :] = jnp.broadcast_to(jnp.sum(total, axis=1, keepdims=True), (32, 128))
 
-    step4(1)
-    step4(2)
-    step4(3)
+    step3(1)
     step4(6)
 
     @pl.loop(0, 4)
@@ -293,6 +291,7 @@
         lane = lax.broadcasted_iota(jnp.int32, (64, 128), 1)
         at[low, :] = jnp.where(lane < 64, a, b).astype(BF)
 
+    step4(1)
     both(1)
     for cc in range(CAND):
         part[0, cc // 4, :, pl.ds(256 * (cc % 4), 256)] = jnp.dot(
@@ -310,7 +309,7 @@
 
     my_rows = pl.ds(pl.multiple_of(64 * y + 16 * z, 16), 16)
 
-    def reduce_sums(p):
+    def reduce_sums(p, meanwhile):
         def go(n, src, dst, tok):
             send(src, dst, rs_send.at[p, n], rs_recv.at[p, n], tok, c)
 
@@ -318,6 +317,7 @@
         go(1, part.at[p, 1, y_rows(2)], ryf.at[p, 1], tm)
         go(2, part.at[p, 1, y_rows(1)], ryd.at[p, 1], ty)
         go(3, part.at[p, 0, y_rows(3)], ryd.at[p, 0], tm)
+        meanwhile()
         landed(ryf.at[p, 0], rs_recv.at[p, 0])
         sy[p, 0] = (ryf[p, 0].astype(F32) + part[p, 0, y_rows(1)].astype(F32)).astype(BF)
         go(4, sy.at[p, 0], rya.at[p, 0], ty)
@@ -380,36 +380,39 @@
         landed(nf.at[p, 0, y_rows(2), :], ag_recv.at[p, 6])
         landed(nf.at[p, 1, y_rows(2), :], ag_recv.at[p, 7])
 
+    def later():
+        step3(2)
+        step3(3)
+        step1(4)
+
     mine = xv[2 * y + lax.div(z, 2), pl.ds(pl.multiple_of(16 * lax.rem(z, 2), 16), 16), :]
-    ac[...] = mine.astype(F32) + reduce_sums(0)
+    ac[...] = mine.astype(F32) + reduce_sums(0, later)
+    step4(2)
+    step4(3)
+    spread(0, rms(ac[...], gain2[...]).astype(BF))
     step2(4)
-    spread(0, rms(ac[...], gain2[...]).astype(BF))
-    step3(4)
     both(2)
     both(3)
 
     @pl.loop(0, 4)
     def _(r):
         rows = pl.ds(pl.multiple_of(64 * r, 64), 64)
-        for h in range(2):
-            o = jnp.dot(
-                nf[0, 0, rows, :], wi[h, pl.ds(0, HALF), :], preferred_element_type=F32
-            ) + jnp.dot(
-                nf[0, 1, rows, :], wi[h, pl.ds(HALF, HALF), :], preferred_element_type=F32
-            )
-            hid[h, rows, :] = (gelu(o[:, :160]) * o[:, 160:320]).astype(BF)
+        gate = up = jnp.zeros((64, 320), F32)
         for cc in range(CAND):
-            part[1, cc // 4, rows, pl.ds(256 * (cc % 4), 256)] = (
-                jnp.dot(hid[0, rows, :], fo[cc, pl.ds(0, 160), :], preferred_element_type=F32)
-                + jnp.dot(hid[1, rows, :], fo[cc, pl.ds(160, 160), :], preferred_element_type=F32)
+            block = nf[0, cc // 4, rows, pl.ds(256 * (cc % 4), 256)]
+            gate = gate + dot_t(block, wi[0, cc])
+            up = up + dot_t(block, wi[1, cc])
+        hid[rows, :] = (gelu(gate) * up).astype(BF)
+        for cc in range(CAND):
+            part[1, cc // 4, rows, pl.ds(256 * (cc % 4), 256)] = jnp.dot(
+                hid[rows, :], fo[cc], preferred_element_type=F32
             ).astype(BF)
 
-    after = ac[...] + reduce_sums(1)
+    after = ac[...] + reduce_sums(1, lambda: step3(4))
     step4(4)
     spread(1, rms(after, gain3[...]).astype(BF))
     both(4)
 
-    width = wv.shape[2]
     ids = gold[k].astype(F32)
     eye = lax.broadcasted_iota(jnp.int32, (32, 32), 0) == lax.broadcasted_iota(jnp.int32, (32, 32), 1)
     start = [((2 * j + h) * width).astype(F32) for h in range(2)]
@@ -426,10 +429,10 @@
         wanted = st[rows, :][:, :1]
         logits = []
         for h in range(2):
-            logits.append(
-                jnp.dot(nf[1, 0, rows, :], wv[h, pl.ds(0, HALF), :], preferred_element_type=F32)
-                + jnp.dot(nf[1, 1, rows, :], wv[h, pl.ds(HALF, HALF), :], preferred_element_type=F32)
-            )
+            one = jnp.zeros((64, width), F32)
+            for cc in range(CAND):
+                one = one + dot_t(nf[1, cc // 4, rows, pl.ds(256 * (cc % 4), 256)], wv[h, cc])
+            logits.append(one)
         high = jnp.maximum(
             jnp.max(logits[0], axis=1, keepdims=True), jnp.max(logits[1], axis=1, keepdims=True)
         )
@@ -494,7 +497,7 @@
     for n in range(7):
         at_ = places[n]
         for slot in range(9):
-            landed(at_(c) if slot < 5 else at_(c, 0), g_send.at[n, slot])
+            landed(at_(c) if slot < 5 else at_(c, (slot - 5) % 2), g_send.at[n, slot])
         if n < 5:
             landed(whole[n](k), g_dsend.at[n])
     for p in range(2):
@@ -516,7 +519,6 @@
 ):
     units = w_in_gate.shape[1]
     width = w_vocab.shape[1]
-    w_in = jnp.concatenate([w_in_gate, w_in_up], axis=1)
     anywhere = pl.BlockSpec(memory_space=pl.ANY)
     vmem = pl.BlockSpec(memory_space=pltpu.VMEM)
     smem = pl.BlockSpec(memory_space=pltpu.SMEM)
@@ -530,7 +532,7 @@
         ),
         in_specs=[
             anywhere, anywhere, anywhere, smem, smem, vmem, vmem, anywhere, anywhere, vmem,
-            anywhere, anywhere, vmem, anywhere,
+            anywhere, anywhere, anywhere, vmem, anywhere,
         ],
         out_specs=(vmem, smem),
         scratch_shapes=[
@@ -542,11 +544,11 @@
             pltpu.VMEM((8, 2 * ROWS, 512), F32),
             pltpu.VMEM((2 * ROWS, 4096), BF),
             pltpu.VMEM((ROWS, 128), BF),
-            pltpu.VMEM((2, D, 64), BF),
             pltpu.VMEM((8, 128, 256), BF),
-            pltpu.VMEM((2, D, 2 * units), BF),
+            pltpu.VMEM((8, 128, 256), BF),
+            pltpu.VMEM((2, 8, 2 * units, 256), BF),
             pltpu.VMEM((8, 2 * units, 256), BF),
-            pltpu.VMEM((2, D, width), BF),
+            pltpu.VMEM((2, 8, width, 256), BF),
             pltpu.VMEM((2, 2, ROWS, HALF), BF),
             pltpu.VMEM((2, 2, 64, HALF), BF),
             pltpu.VMEM((2, 2, 64, HALF), BF),
@@ -559,7 +561,7 @@
             pltpu.VMEM((2, 2, 16, HALF), BF),
             pltpu.VMEM((16, D), F32),
             pltpu.VMEM((2, 2, ROWS, HALF), BF),
-            pltpu.VMEM((2, ROWS, units), BF),
+            pltpu.VMEM((ROWS, 2 * units), BF),
             pltpu.VMEM((2 * ROWS, 128), F32),
             pltpu.VMEM((16, 8, ROWS), F32),
             pltpu.VMEM((16, 8, 128), F32),
@@ -571,8 +573,9 @@
         ),
     )(
         dec_hidden, enc_keys, enc_values, enc_lengths, cand_counts, gold_ids,
-        gain_cross.reshape(1, -1), w_query, w_out, gain_ffn.reshape(1, -1), w_in, w_ffn_out,
-        gain_final.reshape(1, -1), w_vocab,
+        gain_cross.reshape(1, -1), w_query.T, w_out, gain_ffn.reshape(1, -1), w_in_gate.T, w_in_up.T,
+        w_ffn_out,
+        gain_final.reshape(1, -1), w_vocab.T,
     )
 
 

time: 184 us -> 168 us (0.913)
  Pallas kernels: 175 us -> 165 us
  local copies, waits for them, and re-layouts: 7.84 us -> 2.36 us
    pallas_call x1, Pallas kernels: 175 us -> 165 us  [body(): pl.pallas_call(kernel, name='layer', out_shape=(jax.ShapeDtypeStruct((2,...]
    unnamed x6 -> x2, local copies, waits for them, and re-layouts: 7.84 us -> 2.36 us
where the time goes in v2:
time: 168 us
  Pallas kernels  165 us (98%)
  local copies, waits for them, and re-layouts  2.36 us (1%)
    pallas_call x1, Pallas kernels, body(): pl.pallas_call(kernel, name='layer', out_shape=(jax.ShapeDtypeStruct((2,...  165 us

profile of v2, /device:TPU:1, one launch (start us, length us, event | category | flops | bytes accessed | tf_op | source)
XLA Modules:
  0.0 168.1 jit_solution(15658061985045158999)
XLA Ops:
  0.6 165.1 %layer.1 = (f32[2,8]{1,0:T(2,128)}, f32[2]{0:T(128)}) custom-call(bf16[2,8,32,2048]{3,2,1,0:T(8,128)(2,1)} %x_in.1, bf16[2,128,2048]{2,1,0:T(8,128)(2,1)} %keys.1, bf16[2,128,2048]{2,1,0:T(8,128)(2,1)} %vals.1, s32[2]{0:T(128)} %lens.1, s32[2]{0:T(128)} %counts.1, s32[2,8,32]{2,1,0:T(8,128)} %gold.1, f32[1,2048]{1,0:T(1,128)} %bitcast.11, ...), custom_call_target="tpu_custom_call" | custom-call | tf_op jit(solution)/shard_map/layer/pallas_call | solution.py:526
  165.8 1.2 copy.19
  167.0 1.1 copy.20

commit v3 on v2

--- a/solution.py
+++ b/solution.py
@@ -138,24 +138,37 @@
     def g_send_to(n, slot, src, dst, cand):
         send(src, dst, g_send.at[n, slot], g_recv.at[n, slot], t, cand)
 
+    def step1z(n):
+        here = places[n](c)
+        if n < 5:
+            landed(here, g_own.at[n])
+        g_send_to(n, 0, here, here, cz)
+
+    def step1x(n):
+        here = places[n](c)
+        g_send_to(n, 1, here, here, cp)
+        g_send_to(n, 2, here, here, cm)
+
     def step1(n):
-        at_ = places[n]
-        src = at_(c)
-        if n < 5:
-            landed(src, g_own.at[n])
-        g_send_to(n, 0, src, at_(c), cz)
-        g_send_to(n, 1, src, at_(c), cp)
-        g_send_to(n, 2, src, at_(c), cm)
-
-    def step2(n):
+        step1z(n)
+        step1x(n)
+
+    def step2a(n):
         at_ = places[n]
         landed(at_(cz), g_recv.at[n, 0])
         g_send_to(n, 3, at_(cz), at_(cz), cp)
         g_send_to(n, 4, at_(cz), at_(cz), cm)
+
+    def step2b(n):
+        at_ = places[n]
         landed(at_(cm), g_recv.at[n, 1])
         g_send_to(n, 5, at_(cm, 0), at_(cm, 0), cp)
         landed(at_(cp), g_recv.at[n, 2])
         g_send_to(n, 6, at_(cp, 1), at_(cp, 1), cm)
+
+    def step2(n):
+        step2a(n)
+        step2b(n)
 
     def step3(n):
         at_ = places[n]
@@ -225,6 +238,7 @@
     step1(5)
     kv_mine(1)
     step1(6)
+    step1z(4)
     both(0)
     zero = jnp.zeros((ROWS, 64), BF)
     query = jnp.zeros((ROWS, 128), F32)
@@ -307,96 +321,143 @@
     def z_rows(dz):
         return pl.ds(pl.multiple_of(16 * lax.rem(z + dz, NZ), 16), 16)
 
-    my_rows = pl.ds(pl.multiple_of(64 * y + 16 * z, 16), 16)
-
-    def reduce_sums(p, meanwhile):
-        def go(n, src, dst, tok):
-            send(src, dst, rs_send.at[p, n], rs_recv.at[p, n], tok, c)
-
-        go(0, part.at[p, 0, y_rows(2)], ryf.at[p, 0], ty)
-        go(1, part.at[p, 1, y_rows(2)], ryf.at[p, 1], tm)
-        go(2, part.at[p, 1, y_rows(1)], ryd.at[p, 1], ty)
-        go(3, part.at[p, 0, y_rows(3)], ryd.at[p, 0], tm)
-        meanwhile()
-        landed(ryf.at[p, 0], rs_recv.at[p, 0])
-        sy[p, 0] = (ryf[p, 0].astype(F32) + part[p, 0, y_rows(1)].astype(F32)).astype(BF)
-        go(4, sy.at[p, 0], rya.at[p, 0], ty)
-        landed(ryf.at[p, 1], rs_recv.at[p, 1])
-        sy[p, 1] = (ryf[p, 1].astype(F32) + part[p, 1, y_rows(3)].astype(F32)).astype(BF)
-        go(5, sy.at[p, 1], rya.at[p, 1], tm)
-        landed(ryd.at[p, 1], rs_recv.at[p, 2])
-        landed(ryd.at[p, 0], rs_recv.at[p, 3])
-        for h in range(2):
-            landed(rya.at[p, h], rs_recv.at[p, 4 + h])
-            by[p, h] = (
-                rya[p, h].astype(F32) + ryd[p, h].astype(F32)
-                + part[p, h, y_rows(0)].astype(F32)
-            ).astype(BF)
-        go(6, by.at[p, 0, z_rows(2)], rzf.at[p, 0], tz)
-        go(7, by.at[p, 1, z_rows(2)], rzf.at[p, 1], tn)
-        go(8, by.at[p, 1, z_rows(1)], rzd.at[p, 1], tz)
-        go(9, by.at[p, 0, z_rows(3)], rzd.at[p, 0], tn)
-        landed(rzf.at[p, 0], rs_recv.at[p, 6])
-        sz[p, 0] = (rzf[p, 0].astype(F32) + by[p, 0, z_rows(1)].astype(F32)).astype(BF)
-        go(10, sz.at[p, 0], rza.at[p, 0], tz)
-        landed(rzf.at[p, 1], rs_recv.at[p, 7])
-        sz[p, 1] = (rzf[p, 1].astype(F32) + by[p, 1, z_rows(3)].astype(F32)).astype(BF)
-        go(11, sz.at[p, 1], rza.at[p, 1], tn)
-        landed(rzd.at[p, 1], rs_recv.at[p, 8])
-        landed(rzd.at[p, 0], rs_recv.at[p, 9])
+    def yz_rows(dy, dz):
+        at_row = 64 * lax.rem(y + dy, NY) + 16 * lax.rem(z + dz, NZ)
+        return pl.ds(pl.multiple_of(at_row, 16), 16)
+
+    order = (2, 1, 3, 0)
+
+    def rs_go(p, n, src, dst, tok):
+        send(src, dst, rs_send.at[p, n], rs_recv.at[p, n], tok, c)
+
+    def sums_far(p):
+        for dz in order:
+            rs_go(p, dz, part.at[p, 0, yz_rows(2, dz)], ryf.at[p, 0, z_rows(dz)], ty)
+            rs_go(p, 4 + dz, part.at[p, 1, yz_rows(2, dz)], ryf.at[p, 1, z_rows(dz)], tm)
+
+    def sums_up(p):
+        for dz in order:
+            rs_go(p, 8 + dz, part.at[p, 1, yz_rows(1, dz)], ryd.at[p, 1, z_rows(dz)], ty)
+
+    def sums_down(p):
+        for dz in order:
+            rs_go(p, 12 + dz, part.at[p, 0, yz_rows(3, dz)], ryd.at[p, 0, z_rows(dz)], tm)
+
+    def add(out, *terms):
+        total = terms[0].astype(F32)
+        for term in terms[1:]:
+            total = total + term.astype(F32)
+        out[...] = total.astype(BF)
+
+    def sums_end(p):
+        for dz in order:
+            zr = z_rows(dz)
+            landed(ryf.at[p, 0, zr], rs_recv.at[p, dz])
+            add(sy.at[p, 0, zr], ryf[p, 0, zr], part[p, 0, yz_rows(1, dz)])
+            rs_go(p, 16 + dz, sy.at[p, 0, zr], rya.at[p, 0, zr], ty)
+            landed(ryf.at[p, 1, zr], rs_recv.at[p, 4 + dz])
+            add(sy.at[p, 1, zr], ryf[p, 1, zr], part[p, 1, yz_rows(3, dz)])
+            rs_go(p, 20 + dz, sy.at[p, 1, zr], rya.at[p, 1, zr], tm)
+        for dz in order:
+            zr = z_rows(dz)
+            landed(ryd.at[p, 0, zr], rs_recv.at[p, 12 + dz])
+            landed(ryd.at[p, 1, zr], rs_recv.at[p, 8 + dz])
+            for h in range(2):
+                landed(rya.at[p, h, zr], rs_recv.at[p, 16 + 4 * h + dz])
+                add(by.at[p, h, zr], rya[p, h, zr], ryd[p, h, zr], part[p, h, yz_rows(0, dz)])
+            if dz == 2:
+                rs_go(p, 24, by.at[p, 0, zr], rzf.at[p, 0], tz)
+                rs_go(p, 25, by.at[p, 1, zr], rzf.at[p, 1], tn)
+            elif dz == 1:
+                rs_go(p, 26, by.at[p, 1, zr], rzd.at[p, 1], tz)
+            elif dz == 3:
+                rs_go(p, 27, by.at[p, 0, zr], rzd.at[p, 0], tn)
+        landed(rzf.at[p, 0], rs_recv.at[p, 24])
+        add(sz.at[p, 0], rzf[p, 0], by[p, 0, z_rows(1)])
+        rs_go(p, 28, sz.at[p, 0], rza.at[p, 0], tz)
+        landed(rzf.at[p, 1], rs_recv.at[p, 25])
+        add(sz.at[p, 1], rzf[p, 1], by[p, 1, z_rows(3)])
+        rs_go(p, 29, sz.at[p, 1], rza.at[p, 1], tn)
+        landed(rzd.at[p, 1], rs_recv.at[p, 26])
+        landed(rzd.at[p, 0], rs_recv.at[p, 27])
         sums = []
         for h in range(2):
-            landed(rza.at[p, h], rs_recv.at[p, 10 + h])
+            landed(rza.at[p, h], rs_recv.at[p, 28 + h])
             sums.append(
-                rza[p, h].astype(F32) + rzd[p, h].astype(F32)
-                + by[p, h, z_rows(0)].astype(F32)
+                rza[p, h].astype(F32) + rzd[p, h].astype(F32) + by[p, h, z_rows(0)].astype(F32)
             )
         return jnp.concatenate(sums, axis=1)
 
-    def spread(p, value):
-        nf[p, 0, my_rows, :] = value[:, :HALF]
-        nf[p, 1, my_rows, :] = value[:, HALF:]
-
-        def go(n, where, tok):
-            send(where, where, ag_send.at[p, n], ag_recv.at[p, n], tok, c)
-
-        def z_block(dz):
-            return pl.ds(pl.multiple_of(64 * y + 16 * lax.rem(z + dz, NZ), 16), 16)
-
-        go(0, nf.at[p, :, my_rows, :], tz)
-        go(1, nf.at[p, :, my_rows, :], tn)
-        landed(nf.at[p, :, z_block(3), :], ag_recv.at[p, 0])
-        go(2, nf.at[p, 0, z_block(3), :], tz)
-        landed(nf.at[p, :, z_block(1), :], ag_recv.at[p, 1])
-        go(3, nf.at[p, 1, z_block(1), :], tn)
-        landed(nf.at[p, 0, z_block(2), :], ag_recv.at[p, 2])
-        landed(nf.at[p, 1, z_block(2), :], ag_recv.at[p, 3])
-        go(4, nf.at[p, :, y_rows(0), :], ty)
-        go(5, nf.at[p, :, y_rows(0), :], tm)
-        landed(nf.at[p, :, y_rows(3), :], ag_recv.at[p, 4])
-        go(6, nf.at[p, 0, y_rows(3), :], ty)
-        landed(nf.at[p, :, y_rows(1), :], ag_recv.at[p, 5])
-        go(7, nf.at[p, 1, y_rows(1), :], tm)
-        landed(nf.at[p, 0, y_rows(2), :], ag_recv.at[p, 6])
-        landed(nf.at[p, 1, y_rows(2), :], ag_recv.at[p, 7])
-
-    def later():
-        step3(2)
-        step3(3)
-        step1(4)
-
+    def ag_go(p, n, h, rows, tok):
+        where = nf.at[p, h, rows, :]
+        send(where, where, ag_send.at[p, n], ag_recv.at[p, n], tok, c)
+
+    def ag_wait(p, n, h, rows):
+        landed(nf.at[p, h, rows, :], ag_recv.at[p, n])
+
+    def spread(p, value, work, early, late):
+        nf[p, 0, yz_rows(0, 0), :] = value[:, :HALF]
+        nf[p, 1, yz_rows(0, 0), :] = value[:, HALF:]
+
+        def along_y(dz):
+            rows = yz_rows(0, dz)
+            ag_go(p, dz, 0, rows, ty)
+            ag_go(p, 4 + dz, 1, rows, tm)
+            ag_go(p, 8 + dz, 1, rows, ty)
+            ag_go(p, 12 + dz, 0, rows, tm)
+
+        def onward(dz):
+            ag_wait(p, dz, 0, yz_rows(3, dz))
+            ag_go(p, 16 + dz, 0, yz_rows(3, dz), ty)
+            ag_wait(p, 4 + dz, 1, yz_rows(1, dz))
+            ag_go(p, 20 + dz, 1, yz_rows(1, dz), tm)
+
+        own = yz_rows(0, 0)
+        ag_go(p, 24, 0, own, tz)
+        ag_go(p, 25, 1, own, tn)
+        ag_go(p, 26, 1, own, tz)
+        ag_go(p, 27, 0, own, tn)
+        along_y(0)
+        early()
+        ag_wait(p, 24, 0, yz_rows(0, 3))
+        ag_go(p, 28, 0, yz_rows(0, 3), tz)
+        ag_wait(p, 25, 1, yz_rows(0, 1))
+        ag_go(p, 29, 1, yz_rows(0, 1), tn)
+        ag_wait(p, 26, 1, yz_rows(0, 3))
+        along_y(3)
+        ag_wait(p, 27, 0, yz_rows(0, 1))
+        along_y(1)
+        onward(0)
+        ag_wait(p, 28, 0, yz_rows(0, 2))
+        ag_wait(p, 29, 1, yz_rows(0, 2))
+        along_y(2)
+        late()
+        work(0)
+        for dz in (3, 1, 2):
+            onward(dz)
+        for dz in range(4):
+            ag_wait(p, 8 + dz, 1, yz_rows(3, dz))
+        work(3)
+        for dz in range(4):
+            ag_wait(p, 12 + dz, 0, yz_rows(1, dz))
+        work(1)
+        for dz in range(4):
+            ag_wait(p, 16 + dz, 0, yz_rows(2, dz))
+            ag_wait(p, 20 + dz, 1, yz_rows(2, dz))
+        work(2)
+
+    sums_far(0)
+    sums_up(0)
+    sums_down(0)
+    step3(2)
+    step3(3)
+    step1x(4)
+    step2a(4)
     mine = xv[2 * y + lax.div(z, 2), pl.ds(pl.multiple_of(16 * lax.rem(z, 2), 16), 16), :]
-    ac[...] = mine.astype(F32) + reduce_sums(0, later)
-    step4(2)
-    step4(3)
-    spread(0, rms(ac[...], gain2[...]).astype(BF))
-    step2(4)
-    both(2)
-    both(3)
-
-    @pl.loop(0, 4)
-    def _(r):
-        rows = pl.ds(pl.multiple_of(64 * r, 64), 64)
+    ac[...] = mine.astype(F32) + sums_end(0)
+
+    def feed(dy):
+        rows = y_rows(dy)
         gate = up = jnp.zeros((64, 320), F32)
         for cc in range(CAND):
             block = nf[0, cc // 4, rows, pl.ds(256 * (cc % 4), 256)]
@@ -407,25 +468,40 @@
             part[1, cc // 4, rows, pl.ds(256 * (cc % 4), 256)] = jnp.dot(
                 hid[rows, :], fo[cc], preferred_element_type=F32
             ).astype(BF)
-
-    after = ac[...] + reduce_sums(1, lambda: step3(4))
-    step4(4)
-    spread(1, rms(after, gain3[...]).astype(BF))
-    both(4)
+        if dy == 1:
+            sums_up(1)
+        elif dy == 3:
+            sums_down(1)
+        elif dy == 2:
+            sums_far(1)
+
+    def early_0():
+        step4(2)
+        step4(3)
+
+    def late_0():
+        both(2)
+        both(3)
+        step2b(4)
+
+    spread(0, rms(ac[...], gain2[...]).astype(BF), feed, early_0, late_0)
+    step3(4)
+    after = ac[...] + sums_end(1)
 
     ids = gold[k].astype(F32)
     eye = lax.broadcasted_iota(jnp.int32, (32, 32), 0) == lax.broadcasted_iota(jnp.int32, (32, 32), 1)
     start = [((2 * j + h) * width).astype(F32) for h in range(2)]
 
-    for i in range(8):
-        column = jnp.sum(
-            jnp.where(eye, jnp.broadcast_to(ids[i : i + 1, :], (32, 32)), 0.0), axis=1, keepdims=True
-        )
-        st[pl.ds(32 * i, 32), :] = jnp.broadcast_to(column, (32, 128))
-
-    @pl.loop(0, 4)
-    def _(r):
-        rows = pl.ds(pl.multiple_of(64 * r, 64), 64)
+    def gold_rows():
+        for i in range(8):
+            column = jnp.sum(
+                jnp.where(eye, jnp.broadcast_to(ids[i : i + 1, :], (32, 32)), 0.0),
+                axis=1, keepdims=True,
+            )
+            st[pl.ds(32 * i, 32), :] = jnp.broadcast_to(column, (32, 128))
+
+    def vocab(dy):
+        rows = y_rows(dy)
         wanted = st[rows, :][:, :1]
         logits = []
         for h in range(2):
@@ -445,9 +521,15 @@
                 jnp.where(at_col == wanted, logits[h], 0.0), axis=1, keepdims=True
             )
         lane = lax.broadcasted_iota(jnp.int32, (64, 128), 1)
-        st[pl.ds(pl.multiple_of(256 + 64 * r, 64), 64), :] = jnp.where(
+        st[pl.ds(pl.multiple_of(256 + 64 * lax.rem(y + dy, NY), 64), 64), :] = jnp.where(
             lane == 0, high, jnp.where(lane == 1, total, picked)
         )
+
+    def early_1():
+        step4(4)
+        gold_rows()
+
+    spread(1, rms(after, gain3[...]).astype(BF), vocab, early_1, lambda: both(4))
 
     stats = st[pl.ds(256, 256), :].T
     f1[j] = stats[0:8, :]
@@ -500,15 +582,13 @@
             landed(at_(c) if slot < 5 else at_(c, (slot - 5) % 2), g_send.at[n, slot])
         if n < 5:
             landed(whole[n](k), g_dsend.at[n])
-    for p in range(2):
-        for n in range(6):
-            landed(sy.at[p, 0], rs_send.at[p, n])
-            landed(sz.at[p, 0], rs_send.at[p, 6 + n])
-        for n, ref in enumerate(
-            [nf.at[p, :, my_rows, :]] * 2 + [nf.at[p, 0, my_rows, :]] * 2
-            + [nf.at[p, :, y_rows(0), :]] * 2 + [nf.at[p, 0, y_rows(0), :]] * 2
-        ):
-            landed(ref, ag_send.at[p, n])
+    @pl.loop(0, 2)
+    def _(p):
+        @pl.loop(0, 30)
+        def _(n):
+            landed(sz.at[p, 0], rs_send.at[p, n])
+            landed(sz.at[p, 0], ag_send.at[p, n])
+
     landed(f1.at[pl.ds(0, 15)], f_send.at[0])
     landed(f2.at[pl.ds(0, 15)], f_send.at[1])
 
@@ -566,7 +646,7 @@
             pltpu.VMEM((16, 8, ROWS), F32),
             pltpu.VMEM((16, 8, 128), F32),
             dma((2,)), dma((2,)), dma((7, 9)), dma((7, 9)), dma((5,)), dma((5,)), dma((5,)),
-            dma((2, 12)), dma((2, 12)), dma((2, 8)), dma((2, 8)), dma((2,)), dma((2,)), dma((3,)),
+            dma((2, 30)), dma((2, 30)), dma((2, 30)), dma((2, 30)), dma((2,)), dma((2,)), dma((3,)),
         ],
         compiler_params=pltpu.CompilerParams(
             collective_id=0, has_side_effects=True, vmem_limit_bytes=62 * 1024 * 1024

time: 168 us -> 143 us (0.85)
  Pallas kernels: 165 us -> 140 us
    pallas_call x1, Pallas kernels: 165 us -> 140 us  [body(): pl.pallas_call(kernel, name='layer', out_shape=(jax.ShapeDtypeStruct((2,...]
where the time goes in v3:
time: 143 us
  Pallas kernels  140 us (98%)
  local copies, waits for them, and re-layouts  2.36 us (2%)
    pallas_call x1, Pallas kernels, body(): pl.pallas_call(kernel, name='layer', out_shape=(jax.ShapeDtypeStruct((2,...  140 us

profile of v3, /device:TPU:1, one launch (start us, length us, event | category | flops | bytes accessed | tf_op | source)
XLA Modules:
  0.0 142.9 jit_solution(13191494893843063844)
XLA Ops:
  0.6 139.9 %layer.1 = (f32[2,8]{1,0:T(2,128)}, f32[2]{0:T(128)}) custom-call(bf16[2,8,32,2048]{3,2,1,0:T(8,128)(2,1)} %x_in.1, bf16[2,128,2048]{2,1,0:T(8,128)(2,1)} %keys.1, bf16[2,128,2048]{2,1,0:T(8,128)(2,1)} %vals.1, s32[2]{0:T(128)} %lens.1, s32[2]{0:T(128)} %counts.1, s32[2,8,32]{2,1,0:T(8,128)} %gold.1, f32[1,2048]{1,0:T(1,128)} %bitcast.11, ...), custom_call_target="tpu_custom_call" | custom-call | tf_op jit(solution)/shard_map/layer/pallas_call | solution.py:606
  140.6 1.2 copy.19
  141.8 1.1 copy.20

commit v4 on v3

--- a/solution.py
+++ b/solution.py
@@ -40,10 +40,10 @@
 def kernel(
     x_in, keys, vals, lens, counts, gold, gain1, wq_in, wo_in, gain2, wg_in, wu_in, fo_in, gain3, wv_in,
     scores_out, best_out,
-    xv, nx, q2, kb, vb, sc, pb, at,
+    xv, nx, q2, kb, vb, sc, pb,
     wq, wo, wi, fo, wv,
     part, ryf, ryd, rya, sy, by, rzf, rzd, rza, sz, ac, nf,
-    hid, st, f1, f2,
+    st, f1, f2,
     kv_recv, kv_send, g_recv, g_send, g_own, g_dual, g_dsend,
     rs_recv, rs_send, ag_recv, ag_send, f_recv, f_send, l_sem,
 ):
@@ -202,6 +202,7 @@
     pl.semaphore_wait(barrier, TOK - 1 + 2 * (CAND - 1))
 
     step1(0)
+    step1(1)
 
     for n, (src, dst) in enumerate(((keys, kb), (vals, vb))):
         here = dst.at[pl.ds(512 * c + 16 * t, 16), :]
@@ -229,16 +230,18 @@
         landed(ref.at[pl.ds(0, 496), :], kv_recv.at[n])
 
     step2(0)
+    step2(1)
+    step3(0)
+    step3(1)
+    step1(2)
     step1(3)
-    step3(0)
-    step1(1)
-    step1(2)
-    step4(0)
     kv_mine(0)
     step1(5)
     kv_mine(1)
     step1(6)
     step1z(4)
+    step4(0)
+    step4(1)
     both(0)
     zero = jnp.zeros((ROWS, 64), BF)
     query = jnp.zeros((ROWS, 128), F32)
@@ -263,21 +266,20 @@
             sc[cc, rows, :] = jnp.where(live, s, NEG)
 
     step2(5)
-    step2(6)
     score(c)
-    step3(5)
     score(cz)
     score(cm)
-    step3(6)
-    step2(1)
-    step2(2)
-    step2(3)
+    step3(5)
+    step2(6)
     score(cp)
     score(cmz)
     score(cpz)
     step4(5)
     score(co)
     score(coz)
+    step3(6)
+    step2(2)
+    step2(3)
 
     @pl.loop(0, 16)
     def _(r):
@@ -293,24 +295,8 @@
             pb[rows, pl.ds(512 * cc, 512)] = w.astype(BF)
         st[rows, :] = jnp.broadcast_to(jnp.sum(total, axis=1, keepdims=True), (32, 128))
 
-    step3(1)
+    both(1)
     step4(6)
-
-    @pl.loop(0, 4)
-    def _(r):
-        low = pl.ds(pl.multiple_of(64 * r, 64), 64)
-        upp = pl.ds(pl.multiple_of(64 * r + ROWS, 64), 64)
-        a = jnp.dot(pb[low, :], vb[...], preferred_element_type=F32) / st[low, :]
-        b = jnp.dot(pb[upp, :], vb[...], preferred_element_type=F32) / st[upp, :]
-        lane = lax.broadcasted_iota(jnp.int32, (64, 128), 1)
-        at[low, :] = jnp.where(lane < 64, a, b).astype(BF)
-
-    step4(1)
-    both(1)
-    for cc in range(CAND):
-        part[0, cc // 4, :, pl.ds(256 * (cc % 4), 256)] = jnp.dot(
-            at[...], wo[cc], preferred_element_type=F32
-        ).astype(BF)
 
     ty, tm = tok_of(y + 1, z), tok_of(y + 3, z)
     tz, tn = tok_of(y, z + 1), tok_of(y, z + 3)
@@ -349,7 +335,7 @@
             total = total + term.astype(F32)
         out[...] = total.astype(BF)
 
-    def sums_end(p):
+    def sums_end(p, mid):
         for dz in order:
             zr = z_rows(dz)
             landed(ryf.at[p, 0, zr], rs_recv.at[p, dz])
@@ -358,6 +344,7 @@
             landed(ryf.at[p, 1, zr], rs_recv.at[p, 4 + dz])
             add(sy.at[p, 1, zr], ryf[p, 1, zr], part[p, 1, yz_rows(3, dz)])
             rs_go(p, 20 + dz, sy.at[p, 1, zr], rya.at[p, 1, zr], tm)
+        mid()
         for dz in order:
             zr = z_rows(dz)
             landed(ryd.at[p, 0, zr], rs_recv.at[p, 12 + dz])
@@ -432,47 +419,69 @@
         ag_wait(p, 29, 1, yz_rows(0, 2))
         along_y(2)
         late()
-        work(0)
+        work((0,))
         for dz in (3, 1, 2):
             onward(dz)
         for dz in range(4):
             ag_wait(p, 8 + dz, 1, yz_rows(3, dz))
-        work(3)
-        for dz in range(4):
             ag_wait(p, 12 + dz, 0, yz_rows(1, dz))
-        work(1)
+        work((3, 1))
         for dz in range(4):
             ag_wait(p, 16 + dz, 0, yz_rows(2, dz))
             ag_wait(p, 20 + dz, 1, yz_rows(2, dz))
-        work(2)
-
+        work((2,))
+
+    def blocks(p, cc, dys):
+        pieces = [nf[p, cc // 4, y_rows(dy), pl.ds(256 * (cc % 4), 256)] for dy in dys]
+        return pieces[0] if len(pieces) == 1 else jnp.concatenate(pieces, axis=0)
+
+    def attend(dy):
+        low = y_rows(dy)
+        upp = pl.ds(pl.multiple_of(64 * lax.rem(y + dy, NY) + ROWS, 64), 64)
+        a = jnp.dot(pb[low, :], vb[...], preferred_element_type=F32) / st[low, :]
+        b = jnp.dot(pb[upp, :], vb[...], preferred_element_type=F32) / st[upp, :]
+        lane = lax.broadcasted_iota(jnp.int32, (64, 128), 1)
+        heads = jnp.where(lane < 64, a, b).astype(BF)
+        for cc in range(CAND):
+            part[0, cc // 4, low, pl.ds(256 * (cc % 4), 256)] = jnp.dot(
+                heads, wo[cc], preferred_element_type=F32
+            ).astype(BF)
+
+    attend(2)
     sums_far(0)
+    attend(1)
     sums_up(0)
+    attend(3)
     sums_down(0)
-    step3(2)
-    step3(3)
-    step1x(4)
-    step2a(4)
+    attend(0)
+
+    def mid_0():
+        step3(2)
+        step3(3)
+        step1x(4)
+        step2a(4)
+
     mine = xv[2 * y + lax.div(z, 2), pl.ds(pl.multiple_of(16 * lax.rem(z, 2), 16), 16), :]
-    ac[...] = mine.astype(F32) + sums_end(0)
-
-    def feed(dy):
-        rows = y_rows(dy)
-        gate = up = jnp.zeros((64, 320), F32)
+    ac[...] = mine.astype(F32) + sums_end(0, mid_0)
+
+    def feed(dys):
+        gate = up = jnp.zeros((64 * len(dys), 320), F32)
         for cc in range(CAND):
-            block = nf[0, cc // 4, rows, pl.ds(256 * (cc % 4), 256)]
+            block = blocks(0, cc, dys)
             gate = gate + dot_t(block, wi[0, cc])
             up = up + dot_t(block, wi[1, cc])
-        hid[rows, :] = (gelu(gate) * up).astype(BF)
+        hidden = (gelu(gate) * up).astype(BF)
         for cc in range(CAND):
-            part[1, cc // 4, rows, pl.ds(256 * (cc % 4), 256)] = jnp.dot(
-                hid[rows, :], fo[cc], preferred_element_type=F32
-            ).astype(BF)
-        if dy == 1:
+            down = jnp.dot(hidden, fo[cc], preferred_element_type=F32).astype(BF)
+            for n, dy in enumerate(dys):
+                part[1, cc // 4, y_rows(dy), pl.ds(256 * (cc % 4), 256)] = down[
+                    64 * n : 64 * n + 64
+                ]
+        if len(dys) == 2:
             sums_up(1)
-        elif dy == 3:
             sums_down(1)
-        elif dy == 2:
+            step3(4)
+        elif dys[0] == 2:
             sums_far(1)
 
     def early_0():
@@ -485,8 +494,7 @@
         step2b(4)
 
     spread(0, rms(ac[...], gain2[...]).astype(BF), feed, early_0, late_0)
-    step3(4)
-    after = ac[...] + sums_end(1)
+    after = ac[...] + sums_end(1, lambda: step4(4))
 
     ids = gold[k].astype(F32)
     eye = lax.broadcasted_iota(jnp.int32, (32, 32), 0) == lax.broadcasted_iota(jnp.int32, (32, 32), 1)
@@ -500,33 +508,34 @@
             )
             st[pl.ds(32 * i, 32), :] = jnp.broadcast_to(column, (32, 128))
 
-    def vocab(dy):
-        rows = y_rows(dy)
-        wanted = st[rows, :][:, :1]
+    def vocab(dys):
+        size = 64 * len(dys)
+        wanted = [st[y_rows(dy), :][:, :1] for dy in dys]
+        wanted = wanted[0] if len(dys) == 1 else jnp.concatenate(wanted, axis=0)
         logits = []
         for h in range(2):
-            one = jnp.zeros((64, width), F32)
+            one = jnp.zeros((size, width), F32)
             for cc in range(CAND):
-                one = one + dot_t(nf[1, cc // 4, rows, pl.ds(256 * (cc % 4), 256)], wv[h, cc])
+                one = one + dot_t(blocks(1, cc, dys), wv[h, cc])
             logits.append(one)
         high = jnp.maximum(
             jnp.max(logits[0], axis=1, keepdims=True), jnp.max(logits[1], axis=1, keepdims=True)
         )
-        total = jnp.zeros((64, 1), F32)
-        picked = jnp.zeros((64, 1), F32)
+        total = jnp.zeros((size, 1), F32)
+        picked = jnp.zeros((size, 1), F32)
         for h in range(2):
             total = total + jnp.sum(jnp.exp(logits[h] - high), axis=1, keepdims=True)
-            at_col = lax.broadcasted_iota(jnp.int32, (64, width), 1).astype(F32) + start[h]
+            at_col = lax.broadcasted_iota(jnp.int32, (size, width), 1).astype(F32) + start[h]
             picked = picked + jnp.sum(
                 jnp.where(at_col == wanted, logits[h], 0.0), axis=1, keepdims=True
             )
-        lane = lax.broadcasted_iota(jnp.int32, (64, 128), 1)
-        st[pl.ds(pl.multiple_of(256 + 64 * lax.rem(y + dy, NY), 64), 64), :] = jnp.where(
-            lane == 0, high, jnp.where(lane == 1, total, picked)
-        )
+        lane = lax.broadcasted_iota(jnp.int32, (size, 128), 1)
+        found = jnp.where(lane == 0, high, jnp.where(lane == 1, total, picked))
+        for n, dy in enumerate(dys):
+            at_row = 256 + 64 * lax.rem(y + dy, NY)
+            st[pl.ds(pl.multiple_of(at_row, 64), 64), :] = found[64 * n : 64 * n + 64]
 
     def early_1():
-        step4(4)
         gold_rows()
 
     spread(1, rms(after, gain3[...]).astype(BF), vocab, early_1, lambda: both(4))
@@ -623,7 +632,6 @@
             pltpu.VMEM((4096, 128), BF),
             pltpu.VMEM((8, 2 * ROWS, 512), F32),
             pltpu.VMEM((2 * ROWS, 4096), BF),
-            pltpu.VMEM((ROWS, 128), BF),
             pltpu.VMEM((8, 128, 256), BF),
             pltpu.VMEM((8, 128, 256), BF),
             pltpu.VMEM((2, 8, 2 * units, 256), BF),
@@ -641,7 +649,6 @@
             pltpu.VMEM((2, 2, 16, HALF), BF),
             pltpu.VMEM((16, D), F32),
             pltpu.VMEM((2, 2, ROWS, HALF), BF),
-            pltpu.VMEM((ROWS, 2 * units), BF),
             pltpu.VMEM((2 * ROWS, 128), F32),
             pltpu.VMEM((16, 8, ROWS), F32),
             pltpu.VMEM((16, 8, 128), F32),

time: 143 us -> 134 us (0.937)
  Pallas kernels: 140 us -> 131 us
    pallas_call x1, Pallas kernels: 140 us -> 131 us  [body(): pl.pallas_call(kernel, name='layer', out_shape=(jax.ShapeDtypeStruct((2,...]
where the time goes in v4:
time: 134 us
  Pallas kernels  131 us (98%)
  local copies, waits for them, and re-layouts  2.36 us (2%)
    pallas_call x1, Pallas kernels, body(): pl.pallas_call(kernel, name='layer', out_shape=(jax.ShapeDtypeStruct((2,...  131 us

profile of v4, /device:TPU:1, one launch (start us, length us, event | category | flops | bytes accessed | tf_op | source)
XLA Modules:
  0.0 134.3 jit_solution(10033238975309841023)
XLA Ops:
  0.6 131.3 %layer.1 = (f32[2,8]{1,0:T(2,128)}, f32[2]{0:T(128)}) custom-call(bf16[2,8,32,2048]{3,2,1,0:T(8,128)(2,1)} %x_in.1, bf16[2,128,2048]{2,1,0:T(8,128)(2,1)} %keys.1, bf16[2,128,2048]{2,1,0:T(8,128)(2,1)} %vals.1, s32[2]{0:T(128)} %lens.1, s32[2]{0:T(128)} %counts.1, s32[2,8,32]{2,1,0:T(8,128)} %gold.1, f32[1,2048]{1,0:T(1,128)} %bitcast.11, ...), custom_call_target="tpu_custom_call" | custom-call | tf_op jit(solution)/shard_map/layer/pallas_call | solution.py:615
  132.0 1.2 copy.19
  133.2 1.1 copy.20

commit v5 on v4

--- a/solution.py
+++ b/solution.py
@@ -42,7 +42,7 @@
     scores_out, best_out,
     xv, nx, q2, kb, vb, sc, pb,
     wq, wo, wi, fo, wv,
-    part, ryf, ryd, rya, sy, by, rzf, rzd, rza, sz, ac, nf,
+    part, ry, by, rz, ac, nf,
     st, f1, f2,
     kv_recv, kv_send, g_recv, g_send, g_own, g_dual, g_dsend,
     rs_recv, rs_send, ag_recv, ag_send, f_recv, f_send, l_sem,
@@ -138,10 +138,11 @@
     def g_send_to(n, slot, src, dst, cand):
         send(src, dst, g_send.at[n, slot], g_recv.at[n, slot], t, cand)
 
+    def ready(n):
+        landed(places[n](c), g_own.at[n])
+
     def step1z(n):
         here = places[n](c)
-        if n < 5:
-            landed(here, g_own.at[n])
         g_send_to(n, 0, here, here, cz)
 
     def step1x(n):
@@ -176,6 +177,10 @@
         g_send_to(n, 7, at_(cmz, 0), at_(cmz, 0), cp)
         landed(at_(cpz), g_recv.at[n, 4])
         g_send_to(n, 8, at_(cpz, 1), at_(cpz, 1), cm)
+
+    def across(which):
+        for cc in which:
+            send(v_at(cc), v_at(cc), g_dsend.at[4], g_dual.at[4], partner, c)
 
     def step4(n):
         at_ = places[n]
@@ -184,7 +189,10 @@
         landed(at_(coz, 0), g_recv.at[n, 7])
         landed(at_(coz, 1), g_recv.at[n, 8])
         if n < 5:
-            send(whole[n](k), whole[n](k), g_dsend.at[n], g_dual.at[n], partner, c)
+            if n < 4:
+                send(whole[n](k), whole[n](k), g_dsend.at[n], g_dual.at[n], partner, c)
+            else:
+                across((cmz, cpz, co, coz))
 
     def both(n):
         landed(whole[n](1 - k), g_dual.at[n])
@@ -201,6 +209,8 @@
 
     pl.semaphore_wait(barrier, TOK - 1 + 2 * (CAND - 1))
 
+    ready(0)
+    ready(1)
     step1(0)
     step1(1)
 
@@ -229,16 +239,21 @@
         ).wait()
         landed(ref.at[pl.ds(0, 496), :], kv_recv.at[n])
 
+    ready(2)
+    ready(3)
+    step1x(2)
+    step1x(3)
     step2(0)
     step2(1)
     step3(0)
     step3(1)
-    step1(2)
-    step1(3)
     kv_mine(0)
     step1(5)
     kv_mine(1)
     step1(6)
+    ready(4)
+    step1z(2)
+    step1z(3)
     step1z(4)
     step4(0)
     step4(1)
@@ -253,7 +268,7 @@
 
     length = lens[k]
 
-    def score(cc):
+    def score(cc, opening=False):
         place = lax.broadcasted_iota(jnp.int32, (1, 512), 1)
         token = lax.div(place, 16) * 128 + 16 * cc + lax.rem(place, 16)
         live = token < length
@@ -263,10 +278,15 @@
         def _(r):
             rows = pl.ds(pl.multiple_of(128 * r, 128), 128)
             s = dot_t(q2[rows, :], block)
-            sc[cc, rows, :] = jnp.where(live, s, NEG)
+            s = jnp.where(live, s, NEG)
+            sc[cc, rows, :] = s
+            high = jnp.maximum(
+                jnp.maximum(s[:, :128], s[:, 128:256]), jnp.maximum(s[:, 256:384], s[:, 384:])
+            )
+            st[rows, :] = high if opening else jnp.maximum(st[rows, :], high)
 
     step2(5)
-    score(c)
+    score(c, True)
     score(cz)
     score(cm)
     step3(5)
@@ -284,10 +304,7 @@
     @pl.loop(0, 16)
     def _(r):
         rows = pl.ds(pl.multiple_of(32 * r, 32), 32)
-        high = sc[0, rows, :]
-        for cc in range(1, CAND):
-            high = jnp.maximum(high, sc[cc, rows, :])
-        top = jnp.max(high, axis=1, keepdims=True)
+        top = jnp.max(st[rows, :], axis=1, keepdims=True)
         total = jnp.zeros((32, 512), F32)
         for cc in range(CAND):
             w = jnp.exp(sc[cc, rows, :] - top)
@@ -298,9 +315,6 @@
     both(1)
     step4(6)
 
-    ty, tm = tok_of(y + 1, z), tok_of(y + 3, z)
-    tz, tn = tok_of(y, z + 1), tok_of(y, z + 3)
-
     def y_rows(dy):
         return pl.ds(pl.multiple_of(64 * lax.rem(y + dy, NY), 64), 64)
 
@@ -313,123 +327,62 @@
 
     order = (2, 1, 3, 0)
 
-    def rs_go(p, n, src, dst, tok):
-        send(src, dst, rs_send.at[p, n], rs_recv.at[p, n], tok, c)
-
-    def sums_far(p):
+    def sums_send(p):
         for dz in order:
-            rs_go(p, dz, part.at[p, 0, yz_rows(2, dz)], ryf.at[p, 0, z_rows(dz)], ty)
-            rs_go(p, 4 + dz, part.at[p, 1, yz_rows(2, dz)], ryf.at[p, 1, z_rows(dz)], tm)
-
-    def sums_up(p):
-        for dz in order:
-            rs_go(p, 8 + dz, part.at[p, 1, yz_rows(1, dz)], ryd.at[p, 1, z_rows(dz)], ty)
-
-    def sums_down(p):
-        for dz in order:
-            rs_go(p, 12 + dz, part.at[p, 0, yz_rows(3, dz)], ryd.at[p, 0, z_rows(dz)], tm)
-
-    def add(out, *terms):
-        total = terms[0].astype(F32)
-        for term in terms[1:]:
-            total = total + term.astype(F32)
-        out[...] = total.astype(BF)
-
-    def sums_end(p, mid):
+            for dy in (2, 1, 3):
+                n = 4 * (dy - 1) + dz
+                send(
+                    part.at[p, :, yz_rows(dy, dz), :], ry.at[p, dy - 1, :, z_rows(dz), :],
+                    rs_send.at[p, n], rs_recv.at[p, n], tok_of(y + dy, z), c,
+                )
+
+    def sums_end(p, mid, tail):
         for dz in order:
             zr = z_rows(dz)
-            landed(ryf.at[p, 0, zr], rs_recv.at[p, dz])
-            add(sy.at[p, 0, zr], ryf[p, 0, zr], part[p, 0, yz_rows(1, dz)])
-            rs_go(p, 16 + dz, sy.at[p, 0, zr], rya.at[p, 0, zr], ty)
-            landed(ryf.at[p, 1, zr], rs_recv.at[p, 4 + dz])
-            add(sy.at[p, 1, zr], ryf[p, 1, zr], part[p, 1, yz_rows(3, dz)])
-            rs_go(p, 20 + dz, sy.at[p, 1, zr], rya.at[p, 1, zr], tm)
-        mid()
-        for dz in order:
-            zr = z_rows(dz)
-            landed(ryd.at[p, 0, zr], rs_recv.at[p, 12 + dz])
-            landed(ryd.at[p, 1, zr], rs_recv.at[p, 8 + dz])
-            for h in range(2):
-                landed(rya.at[p, h, zr], rs_recv.at[p, 16 + 4 * h + dz])
-                add(by.at[p, h, zr], rya[p, h, zr], ryd[p, h, zr], part[p, h, yz_rows(0, dz)])
+            total = part[p, :, yz_rows(0, dz), :].astype(F32)
+            for dy in (1, 3, 2):
+                landed(ry.at[p, dy - 1, :, zr, :], rs_recv.at[p, 4 * (dy - 1) + dz])
+                total = total + ry[p, dy - 1, :, zr, :].astype(F32)
+            by[p, :, zr, :] = total.astype(BF)
+            if dz:
+                send(
+                    by.at[p, :, zr, :], rz.at[p, dz - 1], rs_send.at[p, 11 + dz],
+                    rs_recv.at[p, 11 + dz], tok_of(y, z + dz), c,
+                )
             if dz == 2:
-                rs_go(p, 24, by.at[p, 0, zr], rzf.at[p, 0], tz)
-                rs_go(p, 25, by.at[p, 1, zr], rzf.at[p, 1], tn)
-            elif dz == 1:
-                rs_go(p, 26, by.at[p, 1, zr], rzd.at[p, 1], tz)
-            elif dz == 3:
-                rs_go(p, 27, by.at[p, 0, zr], rzd.at[p, 0], tn)
-        landed(rzf.at[p, 0], rs_recv.at[p, 24])
-        add(sz.at[p, 0], rzf[p, 0], by[p, 0, z_rows(1)])
-        rs_go(p, 28, sz.at[p, 0], rza.at[p, 0], tz)
-        landed(rzf.at[p, 1], rs_recv.at[p, 25])
-        add(sz.at[p, 1], rzf[p, 1], by[p, 1, z_rows(3)])
-        rs_go(p, 29, sz.at[p, 1], rza.at[p, 1], tn)
-        landed(rzd.at[p, 1], rs_recv.at[p, 26])
-        landed(rzd.at[p, 0], rs_recv.at[p, 27])
-        sums = []
-        for h in range(2):
-            landed(rza.at[p, h], rs_recv.at[p, 28 + h])
-            sums.append(
-                rza[p, h].astype(F32) + rzd[p, h].astype(F32) + by[p, h, z_rows(0)].astype(F32)
-            )
-        return jnp.concatenate(sums, axis=1)
-
-    def ag_go(p, n, h, rows, tok):
-        where = nf.at[p, h, rows, :]
-        send(where, where, ag_send.at[p, n], ag_recv.at[p, n], tok, c)
-
-    def ag_wait(p, n, h, rows):
-        landed(nf.at[p, h, rows, :], ag_recv.at[p, n])
+                mid()
+        tail()
+        total = by[p, :, z_rows(0), :].astype(F32)
+        for dz in (1, 3, 2):
+            landed(rz.at[p, dz - 1], rs_recv.at[p, 11 + dz])
+            total = total + rz[p, dz - 1].astype(F32)
+        return jnp.concatenate([total[0], total[1]], axis=1)
 
     def spread(p, value, work, early, late):
         nf[p, 0, yz_rows(0, 0), :] = value[:, :HALF]
         nf[p, 1, yz_rows(0, 0), :] = value[:, HALF:]
 
+        def go(n, rows, tok):
+            where = nf.at[p, :, rows, :]
+            send(where, where, ag_send.at[p, n], ag_recv.at[p, n], tok, c)
+
         def along_y(dz):
-            rows = yz_rows(0, dz)
-            ag_go(p, dz, 0, rows, ty)
-            ag_go(p, 4 + dz, 1, rows, tm)
-            ag_go(p, 8 + dz, 1, rows, ty)
-            ag_go(p, 12 + dz, 0, rows, tm)
-
-        def onward(dz):
-            ag_wait(p, dz, 0, yz_rows(3, dz))
-            ag_go(p, 16 + dz, 0, yz_rows(3, dz), ty)
-            ag_wait(p, 4 + dz, 1, yz_rows(1, dz))
-            ag_go(p, 20 + dz, 1, yz_rows(1, dz), tm)
-
-        own = yz_rows(0, 0)
-        ag_go(p, 24, 0, own, tz)
-        ag_go(p, 25, 1, own, tn)
-        ag_go(p, 26, 1, own, tz)
-        ag_go(p, 27, 0, own, tn)
+            for dy in (2, 1, 3):
+                go(4 * (dy - 1) + dz, yz_rows(0, dz), tok_of(y + dy, z))
+
+        for dz in (2, 1, 3):
+            go(11 + dz, yz_rows(0, 0), tok_of(y, z + dz))
         along_y(0)
         early()
-        ag_wait(p, 24, 0, yz_rows(0, 3))
-        ag_go(p, 28, 0, yz_rows(0, 3), tz)
-        ag_wait(p, 25, 1, yz_rows(0, 1))
-        ag_go(p, 29, 1, yz_rows(0, 1), tn)
-        ag_wait(p, 26, 1, yz_rows(0, 3))
-        along_y(3)
-        ag_wait(p, 27, 0, yz_rows(0, 1))
-        along_y(1)
-        onward(0)
-        ag_wait(p, 28, 0, yz_rows(0, 2))
-        ag_wait(p, 29, 1, yz_rows(0, 2))
-        along_y(2)
+        for dz in (1, 3, 2):
+            landed(nf.at[p, :, yz_rows(0, 4 - dz), :], ag_recv.at[p, 11 + dz])
+            along_y(4 - dz)
         late()
         work((0,))
-        for dz in (3, 1, 2):
-            onward(dz)
-        for dz in range(4):
-            ag_wait(p, 8 + dz, 1, yz_rows(3, dz))
-            ag_wait(p, 12 + dz, 0, yz_rows(1, dz))
-        work((3, 1))
-        for dz in range(4):
-            ag_wait(p, 16 + dz, 0, yz_rows(2, dz))
-            ag_wait(p, 20 + dz, 1, yz_rows(2, dz))
-        work((2,))
+        for dz in (0, 3, 1, 2):
+            for dy in (1, 3, 2):
+                landed(nf.at[p, :, yz_rows(4 - dy, dz), :], ag_recv.at[p, 4 * (dy - 1) + dz])
+        work((2, 1, 3))
 
     def blocks(p, cc, dys):
         pieces = [nf[p, cc // 4, y_rows(dy), pl.ds(256 * (cc % 4), 256)] for dy in dys]
@@ -448,11 +401,9 @@
             ).astype(BF)
 
     attend(2)
-    sums_far(0)
     attend(1)
-    sums_up(0)
     attend(3)
-    sums_down(0)
+    sums_send(0)
     attend(0)
 
     def mid_0():
@@ -462,7 +413,7 @@
         step2a(4)
 
     mine = xv[2 * y + lax.div(z, 2), pl.ds(pl.multiple_of(16 * lax.rem(z, 2), 16), 16), :]
-    ac[...] = mine.astype(F32) + sums_end(0, mid_0)
+    ac[...] = mine.astype(F32) + sums_end(0, mid_0, lambda: None)
 
     def feed(dys):
         gate = up = jnp.zeros((64 * len(dys), 320), F32)
@@ -477,12 +428,8 @@
                 part[1, cc // 4, y_rows(dy), pl.ds(256 * (cc % 4), 256)] = down[
                     64 * n : 64 * n + 64
                 ]
-        if len(dys) == 2:
-            sums_up(1)
-            sums_down(1)
-            step3(4)
-        elif dys[0] == 2:
-            sums_far(1)
+        if len(dys) > 1:
+            sums_send(1)
 
     def early_0():
         step4(2)
@@ -494,7 +441,11 @@
         step2b(4)
 
     spread(0, rms(ac[...], gain2[...]).astype(BF), feed, early_0, late_0)
-    after = ac[...] + sums_end(1, lambda: step4(4))
+    def mid_1():
+        step3(4)
+        across((c, cz, cm, cp))
+
+    after = ac[...] + sums_end(1, mid_1, lambda: step4(4))
 
     ids = gold[k].astype(F32)
     eye = lax.broadcasted_iota(jnp.int32, (32, 32), 0) == lax.broadcasted_iota(jnp.int32, (32, 32), 1)
@@ -593,10 +544,10 @@
             landed(whole[n](k), g_dsend.at[n])
     @pl.loop(0, 2)
     def _(p):
-        @pl.loop(0, 30)
+        @pl.loop(0, 15)
         def _(n):
-            landed(sz.at[p, 0], rs_send.at[p, n])
-            landed(sz.at[p, 0], ag_send.at[p, n])
+            landed(rz.at[p, 0], rs_send.at[p, n])
+            landed(rz.at[p, 0], ag_send.at[p, n])
 
     landed(f1.at[pl.ds(0, 15)], f_send.at[0])
     landed(f2.at[pl.ds(0, 15)], f_send.at[1])
@@ -638,22 +589,16 @@
             pltpu.VMEM((8, 2 * units, 256), BF),
             pltpu.VMEM((2, 8, width, 256), BF),
             pltpu.VMEM((2, 2, ROWS, HALF), BF),
+            pltpu.VMEM((2, 3, 2, 64, HALF), BF),
             pltpu.VMEM((2, 2, 64, HALF), BF),
-            pltpu.VMEM((2, 2, 64, HALF), BF),
-            pltpu.VMEM((2, 2, 64, HALF), BF),
-            pltpu.VMEM((2, 2, 64, HALF), BF),
-            pltpu.VMEM((2, 2, 64, HALF), BF),
-            pltpu.VMEM((2, 2, 16, HALF), BF),
-            pltpu.VMEM((2, 2, 16, HALF), BF),
-            pltpu.VMEM((2, 2, 16, HALF), BF),
-            pltpu.VMEM((2, 2, 16, HALF), BF),
+            pltpu.VMEM((2, 3, 2, 16, HALF), BF),
             pltpu.VMEM((16, D), F32),
             pltpu.VMEM((2, 2, ROWS, HALF), BF),
             pltpu.VMEM((2 * ROWS, 128), F32),
             pltpu.VMEM((16, 8, ROWS), F32),
             pltpu.VMEM((16, 8, 128), F32),
             dma((2,)), dma((2,)), dma((7, 9)), dma((7, 9)), dma((5,)), dma((5,)), dma((5,)),
-            dma((2, 30)), dma((2, 30)), dma((2, 30)), dma((2, 30)), dma((2,)), dma((2,)), dma((3,)),
+            dma((2, 15)), dma((2, 15)), dma((2, 15)), dma((2, 15)), dma((2,)), dma((2,)), dma((3,)),
         ],
         compiler_params=pltpu.CompilerParams(
             collective_id=0, has_side_effects=True, vmem_limit_bytes=62 * 1024 * 1024

time: 134 us -> 128 us (0.955)
  Pallas kernels: 131 us -> 124 us
    pallas_call x1, Pallas kernels: 131 us -> 124 us  [body(): pl.pallas_call(kernel, name='layer', out_shape=(jax.ShapeDtypeStruct((2,...]
where the time goes in v5:
time: 128 us; the launch traced here: 127 us
  Pallas kernels  124 us (97%)
  local copies, waits for them, and re-layouts  2.36 us (2%)
    pallas_call x1, Pallas kernels, body(): pl.pallas_call(kernel, name='layer', out_shape=(jax.ShapeDtypeStruct((2,...  124 us

profile of v5, /device:TPU:1, one launch (start us, length us, event | category | flops | bytes accessed | tf_op | source)
XLA Modules:
  0.0 127.4 jit_solution(3552172606262553721)
XLA Ops:
  0.6 124.4 %layer.1 = (f32[2,8]{1,0:T(2,128)}, f32[2]{0:T(128)}) custom-call(bf16[2,8,32,2048]{3,2,1,0:T(8,128)(2,1)} %x_in.1, bf16[2,128,2048]{2,1,0:T(8,128)(2,1)} %keys.1, bf16[2,128,2048]{2,1,0:T(8,128)(2,1)} %vals.1, s32[2]{0:T(128)} %lens.1, s32[2]{0:T(128)} %counts.1, s32[2,8,32]{2,1,0:T(8,128)} %gold.1, f32[1,2048]{1,0:T(1,128)} %bitcast.11, ...), custom_call_target="tpu_custom_call" | custom-call | tf_op jit(solution)/shard_map/layer/pallas_call | solution.py:566
  125.1 1.2 copy.19
  126.3 1.1 copy.20

commit v6 on v5

--- a/solution.py
+++ b/solution.py
@@ -39,7 +39,7 @@
 
 def kernel(
     x_in, keys, vals, lens, counts, gold, gain1, wq_in, wo_in, gain2, wg_in, wu_in, fo_in, gain3, wv_in,
-    scores_out, best_out,
+    out,
     xv, nx, q2, kb, vb, sc, pb,
     wq, wo, wi, fo, wv,
     part, ry, by, rz, ac, nf,
@@ -232,6 +232,35 @@
                 here, kv_send.at[n], kv_recv.at[n], to, c,
             )
 
+    def value_far():
+        for n, cc in enumerate((co, coz)):
+            here = vb.at[pl.ds(512 * cc + 16 * t, 16), :]
+            pltpu.make_async_copy(
+                vals.at[k, pl.ds(16 * cc, 16), pl.ds(pl.multiple_of(128 * j, 128), 128)],
+                here, l_sem.at[3 + n],
+            ).start()
+
+            @pl.loop(1, TOK)
+            def _(d, here=here, cc=cc):
+                to = lax.rem(t + d, TOK)
+                send(
+                    vals.at[
+                        lax.rem(to, 2), pl.ds(16 * cc, 16),
+                        pl.ds(pl.multiple_of(128 * lax.div(to, 2), 128), 128),
+                    ],
+                    here, kv_send.at[2], kv_recv.at[2], to, c,
+                )
+
+    def value_end():
+        for n, cc in enumerate((co, coz)):
+            pltpu.make_async_copy(
+                vb.at[pl.ds(0, 16), :], vb.at[pl.ds(512 * cc + 16 * t, 16), :], l_sem.at[3 + n]
+            ).wait()
+        landed(vb.at[pl.ds(0, 992), :], kv_recv.at[2])
+        at_ = places[6]
+        for slot, came in ((1, cm), (2, cp), (3, cmz), (4, cpz)):
+            landed(at_(came), g_recv.at[6, slot])
+
     def kv_mine(n):
         ref = (kb, vb)[n]
         pltpu.make_async_copy(
@@ -241,8 +270,8 @@
 
     ready(2)
     ready(3)
-    step1x(2)
-    step1x(3)
+    step1(2)
+    step1(3)
     step2(0)
     step2(1)
     step3(0)
@@ -251,9 +280,8 @@
     step1(5)
     kv_mine(1)
     step1(6)
+    value_far()
     ready(4)
-    step1z(2)
-    step1z(3)
     step1z(4)
     step4(0)
     step4(1)
@@ -274,9 +302,8 @@
         live = token < length
         block = kb[pl.ds(pl.multiple_of(512 * cc, 512), 512), :]
 
-        @pl.loop(0, 4)
-        def _(r):
-            rows = pl.ds(pl.multiple_of(128 * r, 128), 128)
+        for r in range(4):
+            rows = pl.ds(128 * r, 128)
             s = dot_t(q2[rows, :], block)
             s = jnp.where(live, s, NEG)
             sc[cc, rows, :] = s
@@ -290,30 +317,28 @@
     score(cz)
     score(cm)
     step3(5)
-    step2(6)
+    step2a(6)
     score(cp)
     score(cmz)
     score(cpz)
     step4(5)
     score(co)
     score(coz)
-    step3(6)
     step2(2)
     step2(3)
 
-    @pl.loop(0, 16)
-    def _(r):
-        rows = pl.ds(pl.multiple_of(32 * r, 32), 32)
+    for r in range(8):
+        rows = pl.ds(64 * r, 64)
         top = jnp.max(st[rows, :], axis=1, keepdims=True)
-        total = jnp.zeros((32, 512), F32)
-        for cc in range(CAND):
-            w = jnp.exp(sc[cc, rows, :] - top)
+        total = jnp.zeros((64, 256), F32)
+        for at in range(16):
+            w = jnp.exp(sc[at // 2, rows, pl.ds(256 * (at % 2), 256)] - top)
             total = total + w
-            pb[rows, pl.ds(512 * cc, 512)] = w.astype(BF)
-        st[rows, :] = jnp.broadcast_to(jnp.sum(total, axis=1, keepdims=True), (32, 128))
+            pb[rows, pl.ds(256 * at, 256)] = w.astype(BF)
+        st[rows, :] = jnp.broadcast_to(jnp.sum(total, axis=1, keepdims=True), (64, 128))
 
     both(1)
-    step4(6)
+    value_end()
 
     def y_rows(dy):
         return pl.ds(pl.multiple_of(64 * lax.rem(y + dy, NY), 64), 64)
@@ -388,23 +413,18 @@
         pieces = [nf[p, cc // 4, y_rows(dy), pl.ds(256 * (cc % 4), 256)] for dy in dys]
         return pieces[0] if len(pieces) == 1 else jnp.concatenate(pieces, axis=0)
 
-    def attend(dy):
-        low = y_rows(dy)
-        upp = pl.ds(pl.multiple_of(64 * lax.rem(y + dy, NY) + ROWS, 64), 64)
-        a = jnp.dot(pb[low, :], vb[...], preferred_element_type=F32) / st[low, :]
-        b = jnp.dot(pb[upp, :], vb[...], preferred_element_type=F32) / st[upp, :]
-        lane = lax.broadcasted_iota(jnp.int32, (64, 128), 1)
-        heads = jnp.where(lane < 64, a, b).astype(BF)
-        for cc in range(CAND):
-            part[0, cc // 4, low, pl.ds(256 * (cc % 4), 256)] = jnp.dot(
-                heads, wo[cc], preferred_element_type=F32
-            ).astype(BF)
-
-    attend(2)
-    attend(1)
-    attend(3)
+    halves = [
+        jnp.dot(pb[pl.ds(ROWS * h, ROWS), :], vb[...], preferred_element_type=F32)
+        / st[pl.ds(ROWS * h, ROWS), :]
+        for h in range(2)
+    ]
+    lane = lax.broadcasted_iota(jnp.int32, (ROWS, 128), 1)
+    attended = jnp.where(lane < 64, halves[0], halves[1]).astype(BF)
+    for cc in range(CAND):
+        part[0, cc // 4, :, pl.ds(256 * (cc % 4), 256)] = jnp.dot(
+            attended, wo[cc], preferred_element_type=F32
+        ).astype(BF)
     sums_send(0)
-    attend(0)
 
     def mid_0():
         step3(2)
@@ -526,19 +546,19 @@
     landed(f2.at[pl.ds(0, 15)], f_recv.at[1])
     lane = lax.broadcasted_iota(jnp.int32, (8, 8, 128), 2)
     cand = lax.broadcasted_iota(jnp.int32, (8, 8, 128), 0) * 8 + lane
+    own_lane = lax.broadcasted_iota(jnp.int32, (1, 128), 1)
     for b in range(2):
         count = counts[b]
         inside = jnp.where((cand < count) & (lane < 8), f2[pl.ds(8 * b, 8)], NEG)
-        best_out[b] = jnp.max(inside)
-        own_lane = lax.broadcasted_iota(jnp.int32, (1, 128), 1)
-        own = f2[8 * b + c][0:1, :]
-        scores_out[pl.ds(b, 1), :] = jnp.where(own_lane + 8 * c < count, own, 0.0)[:, :8]
+        own = jnp.where(own_lane + 8 * c < count, f2[8 * b + c][0:1, :], 0.0)
+        out[pl.ds(b, 1), :] = jnp.where(own_lane < 8, own, jnp.max(inside))
 
     for n in range(2):
         landed(kb.at[pl.ds(0, 496), :], kv_send.at[n])
+    landed(kb.at[pl.ds(0, 992), :], kv_send.at[2])
     for n in range(7):
         at_ = places[n]
-        for slot in range(9):
+        for slot in range(5 if n == 6 else 9):
             landed(at_(c) if slot < 5 else at_(c, (slot - 5) % 2), g_send.at[n, slot])
         if n < 5:
             landed(whole[n](k), g_dsend.at[n])
@@ -563,18 +583,15 @@
     vmem = pl.BlockSpec(memory_space=pltpu.VMEM)
     smem = pl.BlockSpec(memory_space=pltpu.SMEM)
     dma = pltpu.SemaphoreType.DMA
-    return pl.pallas_call(
+    found = pl.pallas_call(
         kernel,
         name="layer",
-        out_shape=(
-            jax.ShapeDtypeStruct((2, 8), F32),
-            jax.ShapeDtypeStruct((2,), F32),
-        ),
+        out_shape=jax.ShapeDtypeStruct((2, 128), F32),
         in_specs=[
             anywhere, anywhere, anywhere, smem, smem, vmem, vmem, anywhere, anywhere, vmem,
             anywhere, anywhere, anywhere, vmem, anywhere,
         ],
-        out_specs=(vmem, smem),
+        out_specs=vmem,
         scratch_shapes=[
             pltpu.VMEM((8, 32, D), BF),
             pltpu.VMEM((ROWS, D), BF),
@@ -597,8 +614,8 @@
             pltpu.VMEM((2 * ROWS, 128), F32),
             pltpu.VMEM((16, 8, ROWS), F32),
             pltpu.VMEM((16, 8, 128), F32),
-            dma((2,)), dma((2,)), dma((7, 9)), dma((7, 9)), dma((5,)), dma((5,)), dma((5,)),
-            dma((2, 15)), dma((2, 15)), dma((2, 15)), dma((2, 15)), dma((2,)), dma((2,)), dma((3,)),
+            dma((3,)), dma((3,)), dma((7, 9)), dma((7, 9)), dma((5,)), dma((5,)), dma((5,)),
+            dma((2, 15)), dma((2, 15)), dma((2, 15)), dma((2, 15)), dma((2,)), dma((2,)), dma((5,)),
         ],
         compiler_params=pltpu.CompilerParams(
             collective_id=0, has_side_effects=True, vmem_limit_bytes=62 * 1024 * 1024
@@ -609,6 +626,7 @@
         w_ffn_out,
         gain_final.reshape(1, -1), w_vocab.T,
     )
+    return found[:, :8], found[:, 8]
 
 
 def solution(mesh):

time: 128 us -> 125 us (0.977)
  Pallas kernels: 124 us -> 122 us
    pallas_call x1, Pallas kernels: 124 us -> 122 us  [body(): pl.pallas_call(kernel, name='layer', out_shape=jax.ShapeDtypeStruct((2, 1...]
    slice x0 -> x1, local copies, waits for them, and re-layouts: none -> 1.37 us  [body(): return (found[:, :8], found[:, 8])]
where the time goes in v6:
time: 125 us
  Pallas kernels  122 us (98%)
  local copies, waits for them, and re-layouts  2.62 us (2%)
    pallas_call x1, Pallas kernels, body(): pl.pallas_call(kernel, name='layer', out_shape=jax.ShapeDtypeStruct((2, 1...  122 us

profile of v6, /device:TPU:1, one launch (start us, length us, event | category | flops | bytes accessed | tf_op | source)
XLA Modules:
  0.0 125.3 jit_solution(15587405011102232133)
XLA Ops:
  0.6 122.0 %layer.1 = f32[2,128]{1,0:T(2,128)} custom-call(bf16[2,8,32,2048]{3,2,1,0:T(8,128)(2,1)} %x_in.1, bf16[2,128,2048]{2,1,0:T(8,128)(2,1)} %keys.1, bf16[2,128,2048]{2,1,0:T(8,128)(2,1)} %vals.1, s32[2]{0:T(128)} %lens.1, s32[2]{0:T(128)} %counts.1, s32[2,8,32]{2,1,0:T(8,128)} %gold.1, f32[1,2048]{1,0:T(1,128)} %bitcast.12, bf16[64,256]{1,0:T(8,128)(2,1)} %bitcast.11, ...), custom_call_target="tpu_custom_call" | custom-call | tf_op jit(solution)/shard_map/layer/pallas_call | solution.py:586
  122.6 1.4 %slice_reduce_fusion = f32[2]{0:T(128)} fusion(f32[2,128]{1,0:T(2,128)} %layer.1), kind=kLoop, calls=%fused_computation | loop fusion | bytes 16 | tf_op jit(solution)/shard_map/slice | solution.py:629
  124.0 1.2 copy.18

commit v7 on v6

--- a/solution.py
+++ b/solution.py
@@ -38,14 +38,15 @@
 
 
 def kernel(
-    x_in, keys, vals, lens, counts, gold, gain1, wq_in, wo_in, gain2, wg_in, wu_in, fo_in, gain3, wv_in,
+    x_in, keys, vals, lens_in, counts_in, gold_in, gain1_in, wq_in, wo_in, gain2_in, wg_in, wu_in,
+    fo_in, gain3_in, wv_in,
     out,
     xv, nx, q2, kb, vb, sc, pb,
     wq, wo, wi, fo, wv,
     part, ry, by, rz, ac, nf,
-    st, f1, f2,
+    st, f1, f2, lens, counts, gold, gain1, gain2, gain3,
     kv_recv, kv_send, g_recv, g_send, g_own, g_dual, g_dsend,
-    rs_recv, rs_send, ag_recv, ag_send, f_recv, f_send, l_sem,
+    rs_recv, rs_send, ag_recv, ag_send, f_recv, f_send, l_sem, s_sem,
 ):
     t = lax.axis_index("tok")
     c = lax.axis_index("cand")
@@ -76,6 +77,15 @@
 
     x_copy = pltpu.make_async_copy(x_in.at[k], xv, l_sem.at[0])
     x_copy.start()
+    small = [
+        pltpu.make_async_copy(src, dst, s_sem.at[n])
+        for n, (src, dst) in enumerate((
+            (gain1_in, gain1), (lens_in, lens), (counts_in, counts), (gold_in, gold),
+            (gain2_in, gain2), (gain3_in, gain3),
+        ))
+    ]
+    for copy in small:
+        copy.start()
 
     barrier = pltpu.get_barrier_semaphore()
 
@@ -201,6 +211,8 @@
     own_copies()
 
     x_copy.wait()
+    for copy in small:
+        copy.wait()
 
     @pl.loop(0, 8)
     def _(i):
@@ -581,16 +593,12 @@
     width = w_vocab.shape[1]
     anywhere = pl.BlockSpec(memory_space=pl.ANY)
     vmem = pl.BlockSpec(memory_space=pltpu.VMEM)
-    smem = pl.BlockSpec(memory_space=pltpu.SMEM)
     dma = pltpu.SemaphoreType.DMA
     found = pl.pallas_call(
         kernel,
         name="layer",
         out_shape=jax.ShapeDtypeStruct((2, 128), F32),
-        in_specs=[
-            anywhere, anywhere, anywhere, smem, smem, vmem, vmem, anywhere, anywhere, vmem,
-            anywhere, anywhere, anywhere, vmem, anywhere,
-        ],
+        in_specs=[anywhere] * 15,
         out_specs=vmem,
         scratch_shapes=[
             pltpu.VMEM((8, 32, D), BF),
@@ -614,8 +622,14 @@
             pltpu.VMEM((2 * ROWS, 128), F32),
             pltpu.VMEM((16, 8, ROWS), F32),
             pltpu.VMEM((16, 8, 128), F32),
+            pltpu.SMEM((2,), jnp.int32),
+            pltpu.SMEM((2,), jnp.int32),
+            pltpu.VMEM(gold_ids.shape, jnp.int32),
+            pltpu.VMEM((1, D), F32),
+            pltpu.VMEM((1, D), F32),
+            pltpu.VMEM((1, D), F32),
             dma((3,)), dma((3,)), dma((7, 9)), dma((7, 9)), dma((5,)), dma((5,)), dma((5,)),
-            dma((2, 15)), dma((2, 15)), dma((2, 15)), dma((2, 15)), dma((2,)), dma((2,)), dma((5,)),
+            dma((2, 15)), dma((2, 15)), dma((2, 15)), dma((2, 15)), dma((2,)), dma((2,)), dma((5,)), dma((6,)),
         ],
         compiler_params=pltpu.CompilerParams(
             collective_id=0, has_side_effects=True, vmem_limit_bytes=62 * 1024 * 1024

time: 125 us -> 124 us (level)
  no operation moved by 1% of the time
where the time goes in v7:
time: 124 us
  Pallas kernels  121 us (98%)
  local copies, waits for them, and re-layouts  2.62 us (2%)
    pallas_call x1, Pallas kernels, body(): pl.pallas_call(kernel, name='layer', out_shape=jax.ShapeDtypeStruct((2, 1...  121 us

profile of v7, /device:TPU:1, one launch (start us, length us, event | category | flops | bytes accessed | tf_op | source)
XLA Modules:
  0.0 124.3 jit_solution(15541154731859740129)
XLA Ops:
  0.6 121.1 %layer.1 = f32[2,128]{1,0:T(2,128)} custom-call(bf16[2,8,32,2048]{3,2,1,0:T(8,128)(2,1)} %x_in.1, bf16[2,128,2048]{2,1,0:T(8,128)(2,1)} %keys.1, bf16[2,128,2048]{2,1,0:T(8,128)(2,1)} %vals.1, s32[2]{0:T(128)} %lens_in.1, s32[2]{0:T(128)} %counts_in.1, s32[2,8,32]{2,1,0:T(8,128)} %gold_in.1, f32[1,2048]{1,0:T(1,128)} %bitcast.12, bf16[64,256]{1,0:T(8,128)(2,1)} %bitcast.11, ...), custom_call_target="tpu_custom_call" | custom-call | tf_op jit(solution)/shard_map/layer/pallas_call | solution.py:597
  121.7 1.4 %slice_reduce_fusion = f32[2]{0:T(128)} fusion(f32[2,128]{1,0:T(2,128)} %layer.1), kind=kLoop, calls=%fused_computation | loop fusion | bytes 16 | tf_op jit(solution)/shard_map/slice | solution.py:643
  123.1 1.2 copy.18
